TPU v7x, 32 devices: a whole 2x2x4 slice. The times are simulated.
32 devices in a mesh: gx: 16 (over z, y, x), gy: 2 (over core).
Axes of the slice: x: 2, y: 2, z: 4, core: 2. Of those that a mesh axis runs over, the one named last changes fastest.
Arguments:
- vectors: bfloat16 [4096, 768], P(('gx', 'gy')), may hold values from -6 to 6
- list_ids: int32 [4096], P(('gx', 'gy')), may hold values from 0 to 4095, as said below
- old_order: int32 [4096], replicated, may hold values from 0 to 4095, each once
- new_order: int32 [4096], replicated, may hold values from 0 to 4095, as said below
- centroids: bfloat16 [4096, 768], P('gx', 'gy'), may hold values from -6 to 6
- rotation: bfloat16 [768, 768], replicated, may hold values from -0.21875 to 0.21875
- codebook: bfloat16 [96, 8, 256], P('gy'), may hold values from -8 to 8
Outputs:
- quant_error: float32 [4096, 96], P(('gx', 'gy'))
- list_error: float32 [4096, 96], P('gx', 'gy')
Inputs may be any that keep to these rules, and one draw needn't show every extreme that they name: `list_ids`: owner o holds the lists new_order[o * 256] to new_order[(o + 1) * 256 - 1]. Of the 128 vectors of one device, at most 20 name lists of one owner; in every draw some owner receives exactly 20 vectors from every device that shares its index of gy, and every device sends exactly 20 to some owner. `new_order`: each list once. `old_order`: each list once.
All inputs are finite; a program needn't handle non-finite values.
Results may differ from a plain program's by a relative error of at most 0.012.
Values may be sent and summed in bfloat16 or wider, within the bound.
No kernel may reach another device: no remote copies, remote signals or barrier semaphores. Data moves between devices by JAX's collectives and lax.ppermute only.
A program may use at most 128 MiB of HBM per device.

v0:
```python
import jax
import jax.numpy as jnp
from jax import lax
from jax.sharding import PartitionSpec as P


def subspace_errors(turned, codewords, code_norm):
    row_count = turned.shape[0]
    subspaces, sub_width, code_count = codewords.shape
    group_size = 8
    group_count = subspaces // group_size
    lowered = turned.astype(jnp.bfloat16).reshape(row_count, group_count, group_size, sub_width)
    lowered = jnp.moveaxis(lowered, 1, 0)
    squares = jnp.sum(
        (turned * turned).reshape(row_count, group_count, group_size, sub_width), axis=3
    )
    squares = jnp.moveaxis(squares, 1, 0)
    book_groups = codewords.reshape(group_count, group_size, sub_width, code_count)
    norm_groups = code_norm.reshape(group_count, group_size, code_count)

    def one_group(operands):
        lowered_part, square_part, book_part, norm_part = operands
        inner_terms = jnp.einsum(
            "rgd,gdk->rgk", lowered_part, book_part, preferred_element_type=jnp.float32
        )
        inner_terms = lax.optimization_barrier(inner_terms.astype(jnp.bfloat16)).astype(jnp.float32)
        distance = square_part[:, :, None] - 2.0 * inner_terms + norm_part[None, :, :]
        return jnp.min(distance, axis=2)

    nearest = lax.map(one_group, (lowered, squares, book_groups, norm_groups))
    return jnp.moveaxis(nearest, 0, 1).reshape(row_count, subspaces)


def on_device(vectors, list_ids, old_order, new_order, centroids, rotation, codebook):
    owners = lax.axis_size("gx")
    owner_index = lax.axis_index("gx")
    lists_own = centroids.shape[0]
    list_total = old_order.shape[0]
    rows_dev = vectors.shape[0]
    feature_width = vectors.shape[1]
    capacity = 5 * rows_dev // (2 * owners)
    own_lists = lax.dynamic_slice_in_dim(new_order, owner_index * lists_own, lists_own)
    select = (own_lists[:, None] == old_order[None, :]).astype(jnp.bfloat16)
    own_part = jnp.dot(
        select,
        lax.all_gather(centroids, "gx", axis=0, tiled=True),
        preferred_element_type=jnp.float32,
    )
    own_centroids = lax.all_gather(own_part.astype(jnp.bfloat16), "gy", axis=1, tiled=True)
    rot_cent = jnp.dot(own_centroids, rotation, preferred_element_type=jnp.float32)
    padded_cent = jnp.concatenate([rot_cent, jnp.zeros((1, feature_width), jnp.float32)], axis=0)
    codewords = lax.all_gather(codebook, "gy", axis=0, tiled=True)
    code_float = codewords.astype(jnp.float32)
    code_norm = jnp.sum(code_float * code_float, axis=1)
    subspaces = codewords.shape[0]
    slot_of = (
        jnp.zeros((list_total,), jnp.int32)
        .at[new_order]
        .set(jnp.arange(list_total, dtype=jnp.int32))
    )
    new_slot = slot_of[list_ids]
    dest_owner = new_slot // lists_own
    local_list = new_slot % lists_own
    owner_hits = (dest_owner[:, None] == jnp.arange(owners, dtype=jnp.int32)[None, :]).astype(
        jnp.int32
    )
    before = jnp.cumsum(owner_hits, axis=0) - owner_hits
    position = jnp.sum(before * owner_hits, axis=1)
    target = dest_owner * capacity + position
    labels_flat = jnp.full((owners * capacity,), lists_own, jnp.int32).at[target].set(local_list)
    outgoing = jnp.zeros((owners * capacity, feature_width), jnp.bfloat16).at[target].set(vectors)
    incoming = lax.all_to_all(
        outgoing.reshape(owners, capacity, feature_width),
        "gx",
        split_axis=0,
        concat_axis=0,
        tiled=True,
    )
    labels = lax.all_to_all(
        labels_flat.astype(jnp.bfloat16).reshape(owners, capacity),
        "gx",
        split_axis=0,
        concat_axis=0,
        tiled=True,
    )
    turned = jnp.dot(
        incoming.reshape(-1, feature_width), rotation, preferred_element_type=jnp.float32
    )
    finish_turned = turned
    label_rows = labels.reshape(-1).astype(jnp.int32)
    finish_turned = finish_turned - jnp.take(padded_cent, label_rows, axis=0)
    errors = subspace_errors(finish_turned, codewords, code_norm)
    results = errors.reshape(labels.shape[0], labels.shape[1], subspaces)
    returned = lax.all_to_all(results, "gx", split_axis=0, concat_axis=0, tiled=True)
    quant_error = returned.reshape(owners * capacity, subspaces)[target]
    label_rows = labels.reshape(-1).astype(jnp.int32)
    member = (label_rows[:, None] == jnp.arange(lists_own, dtype=jnp.int32)[None, :]).astype(
        jnp.float32
    )
    list_sums = jnp.einsum(
        "rl,rm->lm", member, results.reshape(-1, subspaces), precision=lax.Precision.HIGHEST
    )
    counts = jnp.sum(member, axis=0)
    list_sums, counts = lax.psum((list_sums, counts), "gy")
    average = list_sums / jnp.maximum(counts, 1.0)[:, None]
    own_columns = subspaces // lax.axis_size("gy")
    list_error = lax.dynamic_slice_in_dim(
        average, lax.axis_index("gy") * own_columns, own_columns, 1
    )
    return (quant_error, list_error)


def solution(mesh):
    in_specs = (
        P(("gx", "gy"), None),
        P(("gx", "gy")),
        P(),
        P(),
        P("gx", "gy"),
        P(),
        P("gy", None, None),
    )
    out_specs = (P(("gx", "gy"), None), P("gx", "gy"))
    return jax.shard_map(
        on_device, mesh=mesh, in_specs=in_specs, out_specs=out_specs, check_vma=False
    )
```

profile of v0, /device:TPU:0, one launch (start us, length us, event | category | flops | bytes accessed | tf_op | source)
XLA Modules:
  0.0 163.8 jit_solution(1331834415479985262)
XLA Ops:
  8.6 15.5 %scatter_custom_fusion = s32[4096]{0:T(1024)S(1)} fusion(s32[4096]{0:T(1024)S(1)} %compare_select_fusion, s32[4096]{0:T(1024)S(1)} %iota.11, s32[]{:T(128)} %copy.34), kind=kCustom, calls=%fused_computation.37 | custom fusion | bytes 16388 | tf_op jit(solution)/shard_map/scatter | solution.py:59
  28.2 8.3 %all-to-all-start.1 = ((bf16[16,1,20]{2,1,0:T(2,128)(2,1)}), bf16[16,1,20]{2,1,0:T(2,128)(2,1)S(1)}, u32[]{:S(2)}, u32[]{:S(2)}) async-start(bf16[16,1,20]{2,1,0:T(2,128)(2,1)} %all_to_all.16), calls=%async_computation.1 | async-start | bytes 16384 | tf_op jit(solution)/shard_map/all_to_all | solution.py:79
  36.5 2.3 %all_gather.11 = bf16[96,8,256]{2,1,0:T(8,128)(2,1)S(1)} all-gather(bf16[48,8,256]{2,1,0:T(8,128)(2,1)} %param.15), channel_id=1, replica_groups=mesh['gx'=16,'gy'=2] {'gy'}, dimensions={0}, use_global_device_ids=true | all-gather | bytes 589824 | tf_op jit(solution)/shard_map/all_gather | solution.py:52
  39.6 1.7 %scatter_custom_fusion.1 = bf16[320,768]{1,0:T(8,128)(2,1)S(1)} fusion(s32[128]{0:T(128)S(1)} %fusion.24, bf16[128,768]{1,0:T(8,128)(2,1)} %param.9, bf16[]{:T(256)} %constant.60.clone.1), kind=kCustom, calls=%fused_computation.27 | custom fusion | bytes 492032 | tf_op jit(solution)/shard_map/scatter | solution.py:71
  42.2 1.6 all-to-all-done.1
  43.8 5.3 %all-to-all-start = ((bf16[16,20,768]{2,1,0:T(8,128)(2,1)}), bf16[16,20,768]{2,1,0:T(8,128)(2,1)S(1)}, u32[]{:S(2)}, u32[]{:S(2)}) async-start(bf16[16,20,768]{2,1,0:T(8,128)(2,1)} %reshape.141), calls=%async_computation | async-start | bytes 1179648 | tf_op jit(solution)/shard_map/all_to_all | solution.py:72
  50.4 2.5 %psum.15 = f32[256]{0:T(256)S(1)} all-reduce(f32[256]{0:T(256)S(1)} %convert_reduce_fusion), channel_id=1, replica_groups=mesh['gx'=16,'gy'=2] {'gy'}, use_global_device_ids=true, to_apply=%region_12.13 | all-reduce | flops 256 | bytes 2048 | tf_op jit(solution)/shard_map/psum | solution.py:104
  52.9 12.6 %all-to-all-done = bf16[16,20,768]{2,1,0:T(8,128)(2,1)S(1)} async-done(((bf16[16,20,768]{2,1,0:T(8,128)(2,1)}), bf16[16,20,768]{2,1,0:T(8,128)(2,1)S(1)}, u32[]{:S(2)}, u32[]{:S(2)}) %all-to-all-start) | async-done | bytes 491552 | tf_op jit(solution)/shard_map/all_to_all | solution.py:72
  66.4 18.4 %all-gather.2.cloned.1.call-done = bf16[4096,384]{1,0:T(8,128)(2,1)} async-done(((bf16[256,384]{1,0:T(8,128)(2,1)}), bf16[4096,384]{1,0:T(8,128)(2,1)}) %all-gather.2.cloned.1.call-update) | async-done | bytes 3145744 | tf_op jit(solution)/shard_map/all_gather | solution.py:46
  84.8 3.2 %fusion.10 = bf16[256,384]{1,0:T(8,128)(2,1)S(1)} fusion(bf16[4096,384]{1,0:T(8,128)(2,1)} %all-gather.2.cloned.1.call-done, s32[4096]{0:T(1024)S(1)} %copy-done.2, s32[256]{0:T(256)S(1)} %dynamic_slice.22), kind=kOutput, calls=%fused_computation.22 | convolution fusion | flops 806453248 | bytes 3359744 | tf_op jit(solution)/shard_map/dot_general | solution.py:44
  88.0 2.1 %all_gather.10 = bf16[256,768]{1,0:T(8,128)(2,1)S(1)} all-gather(bf16[256,384]{1,0:T(8,128)(2,1)S(1)} %fusion.10), channel_id=1, replica_groups=mesh['gx'=16,'gy'=2] {'gy'}, dimensions={1}, use_global_device_ids=true | all-gather | bytes 589824 | tf_op jit(solution)/shard_map/all_gather | solution.py:49
  90.7 1.9 %gather_fusion.1 = f32[320,768]{1,0:T(8,128)S(1)} fusion(f32[257,768]{1,0:T(8,128)S(1)} %concatenate.3, s32[1024]{0:T(1024)S(1)} %pad_clamp_fusion.1), kind=kCustom, calls=%fused_computation.1 | custom fusion | bytes 1967360 | tf_op jit(solution)/shard_map/jit(_take)/gather | solution.py:91
  92.6 2.4 %fusion.25 = (bf16[320,768]{1,0:T(8,128)(2,1)}, f32[320,768]{1,0:T(8,128)S(1)}) fusion(f32[320,768]{1,0:T(8,128)S(1)} %gather_fusion.1, pred[320]{0:T(512)(128)(4,1)S(1)} %compare_and_fusion, bf16[320,768]{1,0:T(8,128)(2,1)} %reshape.142, bf16[768,768]{1,0:T(8,128)(2,1)S(1)} %copy-done), kind=kOutput, calls=%fused_computation.63 | convolution fusion | flops 378470400 | bytes 4129088 | tf_op jit(solution)/shard_map/dot_general | solution.py:86
  95.6 1.3 copy.23
  97.0 39.3 %while.10 = (s32[]{:T(128)}, f32[12,320,8]{1,2,0:T(8,128)S(1)}, f32[12,320,8]{1,2,0:T(8,128)S(1)}, bf16[12,8,8,256]{3,2,1,0:T(8,128)(2,1)}, bf16[12,320,8,8]{1,3...) while((s32[]{:T(128)}, f32[12,320,8]{1,2,0:T(8,128)S(1)}, f32[12,320,8]{1,2,0:T(8,128)S(1)}, ...), condition=%wide.region_9.10_spmd, body=%wide.region_7.9_spmd.sunk | while | flops 14415362 | bytes 2794585 | solution.py:30
  97.0 1.3 fusion.37
  99.0 1.2 add_reduce_fusion.2
  100.2 1.3 fusion.37
  103.5 1.3 fusion.37
  106.8 1.3 fusion.37
  110.1 1.3 fusion.37
  113.3 1.3 fusion.37
  116.6 1.3 fusion.37
  119.9 1.3 fusion.37
  123.1 1.3 fusion.37
  126.4 1.3 fusion.37
  128.5 1.2 add_reduce_fusion.2
  129.7 1.3 fusion.37
  133.0 1.3 fusion.37
  138.7 4.5 %all-to-all-start.2 = ((f32[16,20,96]{2,1,0:T(8,128)}), f32[16,20,96]{2,1,0:T(8,128)S(1)}, u32[]{:S(2)}, u32[]{:S(2)}) async-start(f32[16,20,96]{2,1,0:T(8,128)} %copy.24), calls=%async_computation.2 | async-start | bytes 393216 | tf_op jit(solution)/shard_map/all_to_all | solution.py:94
  143.3 10.8 %all-reduce.3.cloned.1.call-done = f32[256,96]{0,1:T(8,128)} async-done(((f32[256,96]{0,1:T(8,128)}), f32[256,96]{0,1:T(8,128)}) %all-reduce.3.cloned.1.call-update) | async-done | bytes 98320 | tf_op jit(solution)/shard_map/psum | solution.py:104
  154.1 1.4 dynamic-slice_divide_fusion
  (95 shorter events, 34.9 us)
Async XLA Ops:
  7.2 83.0 %copy-start = (bf16[768,768]{1,0:T(8,128)(2,1)S(1)}, bf16[768,768]{1,0:T(8,128)(2,1)}, u32[]{:S(2)}) copy-start(bf16[768,768]{1,0:T(8,128)(2,1)} %param.14) | copy-start | bytes 3538948
  7.2 77.7 %all-gather.2.cloned.1.call-start = ((), (), s32[]{:S(2)}) async-start(), calls=%async_computation.3 | async-start | bytes 3342336 | tf_op jit(solution)/shard_map/all_gather | solution.py:46
  26.1 58.7 %copy-start.2 = (s32[4096]{0:T(1024)S(1)}, s32[4096]{0:T(1024)}, u32[]{:S(2)}) copy-start(s32[4096]{0:T(1024)} %param.11) | copy-start | bytes 49156
  28.2 15.6 %all-to-all-start.1 = ((bf16[16,1,20]{2,1,0:T(2,128)(2,1)}), bf16[16,1,20]{2,1,0:T(2,128)(2,1)S(1)}, u32[]{:S(2)}, u32[]{:S(2)}) async-start(bf16[16,1,20]{2,1,0:T(2,128)(2,1)} %all_to_all.16), calls=%async_computation.1 | async-start | bytes 16384 | tf_op jit(solution)/shard_map/all_to_all | solution.py:79
  38.8 49.2 %copy-start.1 = (bf16[96,8,256]{2,1,0:T(8,128)(2,1)}, bf16[96,8,256]{2,1,0:T(8,128)(2,1)S(1)}, u32[]{:S(2)}) copy-start(bf16[96,8,256]{2,1,0:T(8,128)(2,1)S(1)} %all_gather.11) | copy-start | bytes 1179652
  43.8 21.8 %all-to-all-start = ((bf16[16,20,768]{2,1,0:T(8,128)(2,1)}), bf16[16,20,768]{2,1,0:T(8,128)(2,1)S(1)}, u32[]{:S(2)}, u32[]{:S(2)}) async-start(bf16[16,20,768]{2,1,0:T(8,128)(2,1)} %reshape.141), calls=%async_computation | async-start | bytes 1179648 | tf_op jit(solution)/shard_map/all_to_all | solution.py:72
  49.1 105.0 %all-reduce.3.cloned.1.call-start = ((), (), s32[]{:S(2)}) async-start(), calls=%async_computation.4 | async-start | bytes 196608 | tf_op jit(solution)/shard_map/psum | solution.py:104
  138.7 16.8 %all-to-all-start.2 = ((f32[16,20,96]{2,1,0:T(8,128)}), f32[16,20,96]{2,1,0:T(8,128)S(1)}, u32[]{:S(2)}, u32[]{:S(2)}) async-start(f32[16,20,96]{2,1,0:T(8,128)} %copy.24), calls=%async_computation.2 | async-start | bytes 393216 | tf_op jit(solution)/shard_map/all_to_all | solution.py:94
Sparse Core Ops, SparseCore 0:
  10.8 74.0 all-gather.1
  137.3 16.7 all-reduce.2
where the time goes:
time: 166 us; the launch traced here: 164 us
  waiting for transfers between devices  44.1 us (27%)
  local copies, waits for them, and re-layouts  38 us (23%)
  matrix products  22.8 us (14%)
  other arithmetic  18.9 us (11%)
  starting transfers between devices  18.3 us (11%)
  between operations  14.3 us (9%)
  blocking collectives  6.86 us (4%)
    all_gather x1, waiting for transfers between devices, on_device(): lax.all_gather(centroids, 'gx', axis=0, tiled=True)  18.4 us
    dot_general x12, matrix products, one_group(): jnp.einsum('rgd,gdk->rgk', lowered_part, book_part, preferred_element_typ...  15.8 us
    scatter x1, local copies, waits for them, and re-layouts, on_device(): slot_of = jnp.zeros((list_total,), jnp.int32).at[new_order].set(jnp.arang...  15.5 us
    reduce_min x12, other arithmetic, one_group(): return jnp.min(distance, axis=2)  14.3 us
    all_to_all x1, waiting for transfers between devices, on_device(): lax.all_to_all(outgoing.reshape(owners, capacity, feature_width), 'gx', s...  12.6 us
    psum x1, waiting for transfers between devices, on_device(): list_sums, counts = lax.psum((list_sums, counts), 'gy')  10.8 us
    add x12, local copies, waits for them, and re-layouts, one_group(): square_part[:, :, None] - 2.0 * inner_terms + norm_part[None, :, :]  8.45 us
    all_to_all x1, starting transfers between devices, on_device(): lax.all_to_all(labels_flat.astype(jnp.bfloat16).reshape(owners, capacity)...  8.34 us
  transfers between devices with their start and end apart: 5, of which 4 were waited for; matrix products, arithmetic and copies ran while one was open for 17% of the time, Pallas kernels for 0%

commit v1 on v0

--- a/solution.py
+++ b/solution.py
@@ -1,7 +1,228 @@
+import functools
+
 import jax
 import jax.numpy as jnp
 from jax import lax
+from jax.experimental import pallas as pl
+from jax.experimental.pallas import tpu as pltpu
 from jax.sharding import PartitionSpec as P
+
+LANES = 128
+WIDE = 2 * LANES
+F32 = jnp.float32
+BF16 = jnp.bfloat16
+
+
+def iota_f32(shape, axis):
+    return lax.broadcasted_iota(jnp.int32, shape, axis).astype(F32)
+
+
+def dot(a, b, contract=((1,), (0,))):
+    return lax.dot_general(a, b, (contract, ((), ())), preferred_element_type=F32)
+
+
+def slot_digits(ids_across, order_ref):
+    found = jnp.zeros((LANES, LANES), F32)
+    for block in range(order_ref.shape[0]):
+        found = jnp.where(ids_across == order_ref[block : block + 1, :], float(block + 1), found)
+    hit = (found > 0.0).astype(F32)
+    block_of = (found - hit).astype(BF16)
+    ones = jnp.ones((8, LANES), BF16)
+    lanes = iota_f32((8, LANES), 1).astype(BF16)
+    slot = dot(ones, block_of, ((1,), (1,))) * float(LANES) + dot(lanes, hit.astype(BF16), ((1,), (1,)))
+    high = jnp.floor(slot * (1.0 / WIDE))
+    return high, slot - high * WIDE
+
+
+def prepare_kernel(own, ids_ref, old_ref, new_ref, vec_ref, rot_ref, book_ref, turned_ref, digit_ref, code_ref):
+    ids_across = jnp.broadcast_to(ids_ref[...], (LANES, LANES)).astype(F32).T.astype(jnp.int32)
+    old_high, old_low = slot_digits(ids_across, old_ref)
+    new_high, new_low = slot_digits(ids_across, new_ref)
+    row = lax.broadcasted_iota(jnp.int32, (8, LANES), 0)
+    digits = jnp.where(row == 0, old_high, jnp.where(row == 1, old_low, jnp.where(row == 2, new_high, new_low)))
+    digit_ref[...] = digits.astype(BF16)
+    turned_ref[...] = dot(vec_ref[...], rot_ref[...]).T.astype(BF16)
+    codes = book_ref.shape[2]
+    first = lax.axis_index("gx") * own
+    row = lax.broadcasted_iota(jnp.int32, (8, codes), 0)
+    parts, tails = [], []
+    for m in range(own):
+        words = book_ref[first + m].astype(F32)
+        zero = jnp.zeros_like(words)
+        parts.append(jnp.concatenate([-2.0 * words if n == m else zero for n in range(own)], axis=1))
+        norm = jnp.sum(words * words, axis=0, keepdims=True)
+        top = norm.astype(BF16).astype(F32)
+        middle = (norm - top).astype(BF16).astype(F32)
+        low = norm - top - middle
+        tails.append(jnp.where(row == 0, top, jnp.where(row == 1, middle, jnp.where(row == 2, low, 0.0))))
+    parts.append(jnp.concatenate(tails, axis=1))
+    code_ref[...] = jnp.concatenate(parts, axis=0).T.astype(BF16)
+
+
+def pack_kernel(width, cent_ref, other_ref, rot_ref, turned_ref, digit_ref, out_ref):
+    side = lax.axis_index("gy")
+    half = cent_ref.shape[1]
+    mine = cent_ref[pl.ds(side * LANES, LANES), :]
+    other = other_ref[pl.ds(side * LANES, LANES), :]
+    rotated = dot(mine, rot_ref[pl.ds(side * half, half), :])
+    rotated += dot(other, rot_ref[pl.ds((1 - side) * half, half), :])
+    cents = rotated.T
+    vectors = turned_ref[...].astype(F32)
+    digits = digit_ref[...].astype(F32)
+    for device in range(out_ref.shape[0]):
+        at = (device % 2) * half + (device // 2) * width
+        block = jnp.concatenate([vectors[at : at + width], cents[at : at + width], digits], axis=0)
+        out_ref[device] = block.astype(BF16)
+
+
+def encode_kernel(own, sub_width, in_ref, code_ref, out_ref, table_ref, low_ref, square_ref):
+    devices = in_ref.shape[0]
+    tiles = devices // 2
+    width = own * sub_width
+    codes = code_ref.shape[0] // own
+
+    def pair(tile, lo, hi):
+        return jnp.concatenate([in_ref[2 * tile, lo:hi, :], in_ref[2 * tile + 1, lo:hi, :]], axis=1).astype(F32)
+
+    digits = [pair(tile, 2 * width, 2 * width + 8) for tile in range(tiles)]
+    for tile in range(tiles):
+        table_ref[tile * width : (tile + 1) * width, :] = pair(tile, width, 2 * width)
+    table = table_ref[...].astype(BF16)
+    sub = iota_f32((WIDE, WIDE), 0)
+    tail_row = lax.broadcasted_iota(jnp.int32, (8, WIDE), 0)
+    tail = (tail_row < 3).astype(F32)
+    for tile in range(tiles):
+        hot = (sub == digits[tile][1:2]).astype(F32).astype(BF16)
+        looked = dot(table, hot)
+        high = jnp.broadcast_to(digits[tile][0:1], (width, WIDE))
+        cent = jnp.zeros((width, WIDE), F32)
+        for group in range(tiles):
+            cent = jnp.where(high == float(group), looked[group * width : (group + 1) * width], cent)
+        turned = pair(tile, 0, width) - cent
+        lanes = slice(tile * WIDE, (tile + 1) * WIDE)
+        low_ref[:, lanes] = jnp.concatenate([turned, tail], axis=0).astype(BF16)
+        squared = turned * turned
+        for m in range(own):
+            square_ref[m : m + 1, lanes] = jnp.sum(
+                squared[m * sub_width : (m + 1) * sub_width], axis=0, keepdims=True
+            )
+    code = code_ref[...]
+    sums = jnp.zeros((tiles * 8, WIDE), F32)
+    errors = []
+    for tile in range(tiles):
+        lanes = slice(tile * WIDE, (tile + 1) * WIDE)
+        distance = dot(code, low_ref[:, lanes])
+        nearest = jnp.concatenate(
+            [jnp.min(distance[m * codes : (m + 1) * codes], axis=0, keepdims=True) for m in range(own)], axis=0
+        )
+        error = nearest + square_ref[0:own, lanes]
+        errors.append(error)
+        top = error.astype(BF16).astype(F32)
+        rest = error - top
+        pad = jnp.zeros((8 - 2 * own - 1, WIDE), F32)
+        group_rows = jnp.concatenate([top, rest, jnp.ones((1, WIDE), F32), pad], axis=0)
+        high = jnp.broadcast_to(digits[tile][2:3], (8, WIDE))
+        spread = jnp.concatenate(
+            [jnp.where(high == float(group), group_rows, 0.0) for group in range(tiles)], axis=0
+        ).astype(BF16)
+        hot = (sub == digits[tile][3:4]).astype(F32).astype(BF16)
+        sums = sums + dot(spread, hot, ((1,), (1,)))
+    for tile in range(tiles):
+        group = sums[tile * 8 : (tile + 1) * 8]
+        total = group[0:own] + group[own : 2 * own]
+        mean = total / jnp.maximum(group[2 * own : 2 * own + 1], 1.0)
+        pad = jnp.zeros((out_ref.shape[1] - 3 * own, LANES), F32)
+        for side in range(2):
+            block = jnp.concatenate(
+                [errors[tile][:, side * LANES : (side + 1) * LANES], mean[:, :LANES], mean[:, LANES:], pad], axis=0
+            )
+            out_ref[2 * tile + side] = block.astype(BF16)
+
+
+def finish_kernel(own, in_ref, quant_ref, list_ref, quant_rows, list_rows):
+    tiles = in_ref.shape[0] // 2
+    side = lax.axis_index("gy")
+    for device in range(2 * tiles):
+        at = ((device % 2) * tiles + device // 2) * own
+        quant_rows[at : at + own, :] = in_ref[device].astype(F32)[0:own]
+    for tile in range(tiles):
+        block = in_ref[2 * tile + side].astype(F32)
+        list_rows[tile * own : (tile + 1) * own, 0:LANES] = block[own : 2 * own]
+        list_rows[tile * own : (tile + 1) * own, LANES:WIDE] = block[2 * own : 3 * own]
+    quant_ref[...] = quant_rows[...].T
+    list_ref[...] = list_rows[...].T
+
+
+def on_device_by_column(vectors, list_ids, old_order, new_order, centroids, rotation, codebook):
+    owners, sides = lax.axis_size("gx"), lax.axis_size("gy")
+    devices = owners * sides
+    subspaces, sub_width, codes = codebook.shape
+    own = subspaces // owners
+    width = own * sub_width
+    features = vectors.shape[1]
+    total = subspaces * sides
+    other = lax.ppermute(centroids, "gy", [(0, 1), (1, 0)])
+    turned, digits, code = pl.pallas_call(
+        functools.partial(prepare_kernel, own),
+        out_shape=(
+            jax.ShapeDtypeStruct((features, LANES), BF16),
+            jax.ShapeDtypeStruct((8, LANES), BF16),
+            jax.ShapeDtypeStruct((own * codes, width + 8), BF16),
+        ),
+        name="prepare",
+    )(
+        list_ids.reshape(1, LANES),
+        old_order.reshape(-1, LANES),
+        new_order.reshape(-1, LANES),
+        vectors,
+        rotation,
+        codebook,
+    )
+    outgoing = pl.pallas_call(
+        functools.partial(pack_kernel, width),
+        out_shape=jax.ShapeDtypeStruct((devices, 2 * width + 8, LANES), BF16),
+        name="pack",
+    )(centroids, other, rotation, turned, digits)
+    incoming = lax.all_to_all(outgoing, ("gx", "gy"), split_axis=0, concat_axis=0, tiled=True)
+    returning = pl.pallas_call(
+        functools.partial(encode_kernel, own, sub_width),
+        out_shape=jax.ShapeDtypeStruct((devices, 16, LANES), BF16),
+        scratch_shapes=[
+            pltpu.VMEM((owners * width, WIDE), F32),
+            pltpu.VMEM((width + 8, devices * LANES), BF16),
+            pltpu.VMEM((8, devices * LANES), F32),
+        ],
+        name="encode",
+    )(incoming, code)
+    returned = lax.all_to_all(returning, ("gx", "gy"), split_axis=0, concat_axis=0, tiled=True)
+    return pl.pallas_call(
+        functools.partial(finish_kernel, own),
+        out_shape=(
+            jax.ShapeDtypeStruct((LANES, total), F32),
+            jax.ShapeDtypeStruct((WIDE, subspaces), F32),
+        ),
+        scratch_shapes=[pltpu.VMEM((total, LANES), F32), pltpu.VMEM((subspaces, WIDE), F32)],
+        name="finish",
+    )(returned)
+
+
+def on_device(vectors, list_ids, old_order, new_order, centroids, rotation, codebook):
+    owners, sides = lax.axis_size("gx"), lax.axis_size("gy")
+    subspaces, sub_width, codes = codebook.shape
+    own = subspaces // owners
+    by_column = (
+        sides == 2
+        and own * owners == subspaces
+        and 1 <= own <= 3
+        and sub_width == 8
+        and codes % LANES == 0
+        and vectors.shape[0] == LANES
+        and centroids.shape[0] == WIDE
+        and old_order.shape[0] == owners * WIDE
+        and owners <= WIDE
+    )
+    plan = on_device_by_column if by_column else on_device_by_owner
+    return plan(vectors, list_ids, old_order, new_order, centroids, rotation, codebook)
 
 
 def subspace_errors(turned, codewords, code_norm):
@@ -31,7 +252,7 @@
     return jnp.moveaxis(nearest, 0, 1).reshape(row_count, subspaces)
 
 
-def on_device(vectors, list_ids, old_order, new_order, centroids, rotation, codebook):
+def on_device_by_owner(vectors, list_ids, old_order, new_order, centroids, rotation, codebook):
     owners = lax.axis_size("gx")
     owner_index = lax.axis_index("gx")
     lists_own = centroids.shape[0]

time: 166 us -> 51.6 us (0.31); the launches traced: 164 us -> 51.2 us
  waiting for transfers between devices: 44.1 us -> 0.01 us
  local copies, waits for them, and re-layouts: 38 us -> 3.82 us
  blocking collectives: 6.86 us -> 32.9 us
  matrix products: 22.8 us -> 0 us
  other arithmetic: 18.9 us -> 0 us
  starting transfers between devices: 18.3 us -> 0.56 us
  between operations: 14.3 us -> 0.64 us
  Pallas kernels: 0 us -> 13.2 us
    all_to_all x0 -> x2, blocking collectives: none -> 32.9 us  [the longest x1 21.5 us: on_device_by_column(): lax.all_to_all(outgoing, ('gx', 'gy'), split_axis=0, concat_axis=0, tiled...]
    dot_general x16 -> x0, matrix products: 22.8 us -> none  [the longest x12 15.8 us: one_group(): jnp.einsum('rgd,gdk->rgk', lowered_part, book_part, preferred_element_typ...]
    all_gather x1 -> x0, waiting for transfers between devices: 18.4 us -> none  [on_device(): lax.all_gather(centroids, 'gx', axis=0, tiled=True)]
    all_to_all x3 -> x0, starting transfers between devices: 18.2 us -> none  [the longest x1 8.34 us: on_device(): lax.all_to_all(labels_flat.astype(jnp.bfloat16).reshape(owners, capacity)...]
    scatter x3 -> x0, local copies, waits for them, and re-layouts: 18.2 us -> none  [the longest x1 15.5 us: on_device(): slot_of = jnp.zeros((list_total,), jnp.int32).at[new_order].set(jnp.arang...]
    reduce_min x12 -> x0, other arithmetic: 14.3 us -> none  [one_group(): return jnp.min(distance, axis=2)]
    all_to_all x3 -> x0, waiting for transfers between devices: 14.2 us -> none  [the longest x1 12.6 us: on_device(): lax.all_to_all(outgoing.reshape(owners, capacity, feature_width), 'gx', s...]
    pallas_call x0 -> x4, Pallas kernels: none -> 13.2 us  [the longest x1 5.77 us: on_device_by_column(): pl.pallas_call(functools.partial(encode_kernel, own, sub_width), out_shap...]
  transfers between devices with their start and end apart: 5 -> 1, of which waited for: 4 -> 0; matrix products, arithmetic and copies ran while one was open for 17% -> 0% of each run, Pallas kernels for 0% -> 6%
where the time goes in v1:
time: 51.6 us; the launch traced here: 51.2 us
  blocking collectives  32.9 us (64%)
  Pallas kernels  13.2 us (26%)
  local copies, waits for them, and re-layouts  3.82 us (7%)
  between operations  0.64 us (1%)
  starting transfers between devices  0.56 us (1%)
    all_to_all x1, blocking collectives, on_device_by_column(): lax.all_to_all(outgoing, ('gx', 'gy'), split_axis=0, concat_axis=0, tiled...  21.5 us
    all_to_all x1, blocking collectives, on_device_by_column(): lax.all_to_all(returning, ('gx', 'gy'), split_axis=0, concat_axis=0, tile...  11.4 us
    pallas_call x1, Pallas kernels, on_device_by_column(): pl.pallas_call(functools.partial(encode_kernel, own, sub_width), out_shap...  5.77 us
    pallas_call x2, local copies, waits for them, and re-layouts, on_device_by_column(): pl.pallas_call(functools.partial(finish_kernel, own), out_shape=(jax.Shap...  3.15 us
    pallas_call x1, Pallas kernels, on_device_by_column(): pl.pallas_call(functools.partial(prepare_kernel, own), out_shape=(jax.Sha...  2.96 us
    pallas_call x1, Pallas kernels, on_device_by_column(): pl.pallas_call(functools.partial(pack_kernel, width), out_shape=jax.Shape...  2.8 us
    pallas_call x1, Pallas kernels, on_device_by_column(): pl.pallas_call(functools.partial(finish_kernel, own), out_shape=(jax.Shap...  1.7 us
  transfers between devices with their start and end apart: 1, of which 0 were waited for; matrix products, arithmetic and copies ran while one was open for 0% of the time, Pallas kernels for 6%

profile of v1, /device:TPU:0, one launch (start us, length us, event | category | flops | bytes accessed | tf_op | source)
XLA Modules:
  0.0 51.2 jit_solution(2960801690815676495)
XLA Ops:
  0.6 0.6 %collective-permute-start = (bf16[256,384]{1,0:T(8,128)(2,1)}, bf16[256,384]{1,0:T(8,128)(2,1)S(1)}, u32[]{:S(2)}, u32[]{:S(2)}) collective-permute-start(bf16[256,384]{1,0:T(8,128)(2,1)} %cent_ref.1), channel_id=1, source_target_pairs={{0,1},{1,0},{2,3},{3,2},{4,5},{5,4},{6,7},{7,6},{8,9},{9,8},{10,11... | collective-permute-start | bytes 589832 | tf_op jit(solution)/shard_map/ppermute | solution.py:164
  1.2 3.0 %prepare.1 = (bf16[768,128]{1,0:T(8,128)(2,1)}, bf16[8,128]{1,0:T(8,128)(2,1)}, bf16[768,32]{1,0:T(8,128)(2,1)}) custom-call(s32[1,128]{1,0:T(1,128)} %bitcast.5, s32[32,128]{1,0:T(8,128)} %bitcast.3, s32[32,128]{1,0:T(8,128)} %bitcast.4, bf16[128,768]{1,0:T(8,128)(2,1)} %vec_ref.1, bf16[768,768]{1,0:T(8,128)(2,1)} %rot_ref.3, bf16[48,8,256]{2,1,0:T(8,128)(2,1)} %book_ref.1), custom_call_target="tpu_custom_call" | custom-call | tf_op jit(solution)/shard_map/prepare/pallas_call | solution.py:165
  4.2 0.0 collective-permute-done.other_ref
  4.2 0.0 copy-start
  4.2 0.7 %copy-done = bf16[256,384]{1,0:T(8,128)(2,1)} copy-done((bf16[256,384]{1,0:T(8,128)(2,1)}, bf16[256,384]{1,0:T(8,128)(2,1)S(1)}, u32[]{:S(2)}) %copy-start) | copy-done | bytes 196632
  4.8 2.8 %pack.1 = bf16[32,56,128]{2,1,0:T(8,128)(2,1)} custom-call(bf16[256,384]{1,0:T(8,128)(2,1)} %cent_ref.1, bf16[256,384]{1,0:T(8,128)(2,1)} %copy-done, bf16[768,768]{1,0:T(8,128)(2,1)} %rot_ref.3, bf16[768,128]{1,0:T(8,128)(2,1)} %get-tuple-element.5.turned_ref, bf16[8,128]{1,0:T(8,128)(2,1)} %get-tuple-element.6.digit_ref), custom_call_target="tpu_custom_call" | custom-call | tf_op jit(solution)/shard_map/pack/pallas_call | solution.py:181
  7.6 21.5 %all_to_all.10.in_ref = bf16[32,56,128]{2,1,0:T(8,128)(2,1)} all-to-all(bf16[32,56,128]{2,1,0:T(8,128)(2,1)} %pack.1), channel_id=1, replica_groups=mesh['gx'=16,'gy'=2] {'gx','gy'}, dimensions={0} | all-to-all | bytes 917504 | tf_op jit(solution)/shard_map/all_to_all | solution.py:186
  29.1 5.8 %encode.1 = bf16[32,16,128]{2,1,0:T(8,128)(2,1)} custom-call(bf16[32,56,128]{2,1,0:T(8,128)(2,1)} %all_to_all.10.in_ref, bf16[768,32]{1,0:T(8,128)(2,1)} %get-tuple-element.7.code_ref), custom_call_target="tpu_custom_call" | custom-call | tf_op jit(solution)/shard_map/encode/pallas_call | solution.py:187
  34.9 11.4 %all_to_all.11.in_ref = bf16[32,16,128]{2,1,0:T(8,128)(2,1)} all-to-all(bf16[32,16,128]{2,1,0:T(8,128)(2,1)} %encode.1), channel_id=1, replica_groups=mesh['gx'=16,'gy'=2] {'gx','gy'}, dimensions={0} | all-to-all | bytes 262144 | tf_op jit(solution)/shard_map/all_to_all | solution.py:197
  46.3 1.7 %finish.1 = (f32[128,96]{1,0:T(8,128)}, f32[256,48]{1,0:T(8,128)}) custom-call(bf16[32,16,128]{2,1,0:T(8,128)(2,1)} %all_to_all.11.in_ref), custom_call_target="tpu_custom_call" | custom-call | tf_op jit(solution)/shard_map/finish/pallas_call | solution.py:198
  48.0 1.5 %copy.9 = f32[128,96]{0,1:T(8,128)} copy(f32[128,96]{1,0:T(8,128)} %get-tuple-element.8) | data formatting | bytes 98304 | tf_op jit(solution)/shard_map/finish/pallas_call | solution.py:198
  49.6 1.6 %copy.10 = f32[256,48]{0,1:T(8,128)} copy(f32[256,48]{1,0:T(8,128)} %get-tuple-element.9) | data formatting | bytes 98304 | tf_op jit(solution)/shard_map/finish/pallas_call | solution.py:198
Async XLA Ops:
  0.6 3.5 %collective-permute-start = (bf16[256,384]{1,0:T(8,128)(2,1)}, bf16[256,384]{1,0:T(8,128)(2,1)S(1)}, u32[]{:S(2)}, u32[]{:S(2)}) collective-permute-start(bf16[256,384]{1,0:T(8,128)(2,1)} %cent_ref.1), channel_id=1, source_target_pairs={{0,1},{1,0},{2,3},{3,2},{4,5},{5,4},{6,7},{7,6},{8,9},{9,8},{10,11... | collective-permute-start | bytes 589832 | tf_op jit(solution)/shard_map/ppermute | solution.py:164
  4.2 0.7 %copy-start = (bf16[256,384]{1,0:T(8,128)(2,1)}, bf16[256,384]{1,0:T(8,128)(2,1)S(1)}, u32[]{:S(2)}) copy-start(bf16[256,384]{1,0:T(8,128)(2,1)S(1)} %collective-permute-done.other_ref) | copy-start | bytes 589828

commit v2 on v1

--- a/solution.py
+++ b/solution.py
@@ -11,6 +11,9 @@
 WIDE = 2 * LANES
 F32 = jnp.float32
 BF16 = jnp.bfloat16
+
+
+VMEM = pl.BlockSpec(memory_space=pltpu.VMEM)
 
 
 def iota_f32(shape, axis):
@@ -139,18 +142,16 @@
             out_ref[2 * tile + side] = block.astype(BF16)
 
 
-def finish_kernel(own, in_ref, quant_ref, list_ref, quant_rows, list_rows):
+def finish_kernel(own, in_ref, quant_ref, list_ref):
     tiles = in_ref.shape[0] // 2
     side = lax.axis_index("gy")
     for device in range(2 * tiles):
         at = ((device % 2) * tiles + device // 2) * own
-        quant_rows[at : at + own, :] = in_ref[device].astype(F32)[0:own]
+        quant_ref[at : at + own, :] = in_ref[device].astype(F32)[0:own]
     for tile in range(tiles):
         block = in_ref[2 * tile + side].astype(F32)
-        list_rows[tile * own : (tile + 1) * own, 0:LANES] = block[own : 2 * own]
-        list_rows[tile * own : (tile + 1) * own, LANES:WIDE] = block[2 * own : 3 * own]
-    quant_ref[...] = quant_rows[...].T
-    list_ref[...] = list_rows[...].T
+        list_ref[tile * own : (tile + 1) * own, 0:LANES] = block[own : 2 * own]
+        list_ref[tile * own : (tile + 1) * own, LANES:WIDE] = block[2 * own : 3 * own]
 
 
 def on_device_by_column(vectors, list_ids, old_order, new_order, centroids, rotation, codebook):
@@ -169,6 +170,8 @@
             jax.ShapeDtypeStruct((8, LANES), BF16),
             jax.ShapeDtypeStruct((own * codes, width + 8), BF16),
         ),
+        in_specs=[VMEM] * 6,
+        out_specs=(VMEM, VMEM, VMEM),
         name="prepare",
     )(
         list_ids.reshape(1, LANES),
@@ -181,6 +184,8 @@
     outgoing = pl.pallas_call(
         functools.partial(pack_kernel, width),
         out_shape=jax.ShapeDtypeStruct((devices, 2 * width + 8, LANES), BF16),
+        in_specs=[VMEM] * 5,
+        out_specs=VMEM,
         name="pack",
     )(centroids, other, rotation, turned, digits)
     incoming = lax.all_to_all(outgoing, ("gx", "gy"), split_axis=0, concat_axis=0, tiled=True)
@@ -192,18 +197,22 @@
             pltpu.VMEM((width + 8, devices * LANES), BF16),
             pltpu.VMEM((8, devices * LANES), F32),
         ],
+        in_specs=[VMEM] * 2,
+        out_specs=VMEM,
         name="encode",
     )(incoming, code)
     returned = lax.all_to_all(returning, ("gx", "gy"), split_axis=0, concat_axis=0, tiled=True)
-    return pl.pallas_call(
+    quant_error, list_error = pl.pallas_call(
         functools.partial(finish_kernel, own),
         out_shape=(
-            jax.ShapeDtypeStruct((LANES, total), F32),
-            jax.ShapeDtypeStruct((WIDE, subspaces), F32),
+            jax.ShapeDtypeStruct((total, LANES), F32),
+            jax.ShapeDtypeStruct((subspaces, WIDE), F32),
         ),
-        scratch_shapes=[pltpu.VMEM((total, LANES), F32), pltpu.VMEM((subspaces, WIDE), F32)],
+        in_specs=[VMEM],
+        out_specs=(VMEM, VMEM),
         name="finish",
     )(returned)
+    return quant_error.T, list_error.T
 
 
 def on_device(vectors, list_ids, old_order, new_order, centroids, rotation, codebook):

time: 51.6 us -> 48.2 us (0.934)
  local copies, waits for them, and re-layouts: 3.82 us -> 0.67 us
    pallas_call x2 -> x0, local copies, waits for them, and re-layouts: 3.15 us -> none  [on_device_by_column(): pl.pallas_call(functools.partial(finish_kernel, own), out_shape=(jax.Shap...]
where the time goes in v2:
time: 48.2 us; the launch traced here: 47.9 us
  blocking collectives  32.9 us (68%)
  Pallas kernels  13.1 us (27%)
  local copies, waits for them, and re-layouts  0.67 us (1%)
  between operations  0.64 us (1%)
  starting transfers between devices  0.56 us (1%)
    all_to_all x1, blocking collectives, on_device_by_column(): lax.all_to_all(outgoing, ('gx', 'gy'), split_axis=0, concat_axis=0, tiled...  21.5 us
    all_to_all x1, blocking collectives, on_device_by_column(): lax.all_to_all(returning, ('gx', 'gy'), split_axis=0, concat_axis=0, tile...  11.4 us
    pallas_call x1, Pallas kernels, on_device_by_column(): pl.pallas_call(functools.partial(encode_kernel, own, sub_width), out_shap...  5.77 us
    pallas_call x1, Pallas kernels, on_device_by_column(): pl.pallas_call(functools.partial(prepare_kernel, own), out_shape=(jax.Sha...  2.96 us
    pallas_call x1, Pallas kernels, on_device_by_column(): pl.pallas_call(functools.partial(pack_kernel, width), out_shape=jax.Shape...  2.8 us
    pallas_call x1, Pallas kernels, on_device_by_column(): pl.pallas_call(functools.partial(finish_kernel, own), out_shape=(jax.Shap...  1.55 us
  transfers between devices with their start and end apart: 1, of which 0 were waited for; matrix products, arithmetic and copies ran while one was open for 0% of the time, Pallas kernels for 6%

profile of v2, /device:TPU:0, one launch (start us, length us, event | category | flops | bytes accessed | tf_op | source)
XLA Modules:
  0.0 47.9 jit_solution(14337823665668973696)
XLA Ops:
  0.6 0.6 %collective-permute-start = (bf16[256,384]{1,0:T(8,128)(2,1)}, bf16[256,384]{1,0:T(8,128)(2,1)S(1)}, u32[]{:S(2)}, u32[]{:S(2)}) collective-permute-start(bf16[256,384]{1,0:T(8,128)(2,1)} %cent_ref.1), channel_id=1, source_target_pairs={{0,1},{1,0},{2,3},{3,2},{4,5},{5,4},{6,7},{7,6},{8,9},{9,8},{10,11... | collective-permute-start | bytes 589832 | tf_op jit(solution)/shard_map/ppermute | solution.py:165
  1.2 3.0 %prepare.1 = (bf16[768,128]{1,0:T(8,128)(2,1)}, bf16[8,128]{1,0:T(8,128)(2,1)}, bf16[768,32]{1,0:T(8,128)(2,1)}) custom-call(s32[1,128]{1,0:T(1,128)} %bitcast.7, s32[32,128]{1,0:T(8,128)} %bitcast.5, s32[32,128]{1,0:T(8,128)} %bitcast.6, bf16[128,768]{1,0:T(8,128)(2,1)} %vec_ref.1, bf16[768,768]{1,0:T(8,128)(2,1)} %rot_ref.3, bf16[48,8,256]{2,1,0:T(8,128)(2,1)} %book_ref.1), custom_call_target="tpu_custom_call" | custom-call | tf_op jit(solution)/shard_map/prepare/pallas_call | solution.py:166
  4.2 0.0 collective-permute-done.other_ref
  4.2 0.0 copy-start
  4.2 0.7 %copy-done = bf16[256,384]{1,0:T(8,128)(2,1)} copy-done((bf16[256,384]{1,0:T(8,128)(2,1)}, bf16[256,384]{1,0:T(8,128)(2,1)S(1)}, u32[]{:S(2)}) %copy-start) | copy-done | bytes 196632
  4.8 2.8 %pack.1 = bf16[32,56,128]{2,1,0:T(8,128)(2,1)} custom-call(bf16[256,384]{1,0:T(8,128)(2,1)} %cent_ref.1, bf16[256,384]{1,0:T(8,128)(2,1)} %copy-done, bf16[768,768]{1,0:T(8,128)(2,1)} %rot_ref.3, bf16[768,128]{1,0:T(8,128)(2,1)} %get-tuple-element.7.turned_ref, bf16[8,128]{1,0:T(8,128)(2,1)} %get-tuple-element.8.digit_ref), custom_call_target="tpu_custom_call" | custom-call | tf_op jit(solution)/shard_map/pack/pallas_call | solution.py:184
  7.6 21.5 %all_to_all.10.in_ref = bf16[32,56,128]{2,1,0:T(8,128)(2,1)} all-to-all(bf16[32,56,128]{2,1,0:T(8,128)(2,1)} %pack.1), channel_id=1, replica_groups=mesh['gx'=16,'gy'=2] {'gx','gy'}, dimensions={0} | all-to-all | bytes 917504 | tf_op jit(solution)/shard_map/all_to_all | solution.py:191
  29.1 5.8 %encode.1 = bf16[32,16,128]{2,1,0:T(8,128)(2,1)} custom-call(bf16[32,56,128]{2,1,0:T(8,128)(2,1)} %all_to_all.10.in_ref, bf16[768,32]{1,0:T(8,128)(2,1)} %get-tuple-element.9.code_ref), custom_call_target="tpu_custom_call" | custom-call | tf_op jit(solution)/shard_map/encode/pallas_call | solution.py:192
  34.9 11.4 %all_to_all.11.in_ref = bf16[32,16,128]{2,1,0:T(8,128)(2,1)} all-to-all(bf16[32,16,128]{2,1,0:T(8,128)(2,1)} %encode.1), channel_id=1, replica_groups=mesh['gx'=16,'gy'=2] {'gx','gy'}, dimensions={0} | all-to-all | bytes 262144 | tf_op jit(solution)/shard_map/all_to_all | solution.py:204
  46.3 1.6 %finish.1 = (f32[96,128]{1,0:T(8,128)}, f32[48,256]{1,0:T(8,128)}) custom-call(bf16[32,16,128]{2,1,0:T(8,128)(2,1)} %all_to_all.11.in_ref), custom_call_target="tpu_custom_call" | custom-call | tf_op jit(solution)/shard_map/finish/pallas_call | solution.py:205
Async XLA Ops:
  0.6 3.5 %collective-permute-start = (bf16[256,384]{1,0:T(8,128)(2,1)}, bf16[256,384]{1,0:T(8,128)(2,1)S(1)}, u32[]{:S(2)}, u32[]{:S(2)}) collective-permute-start(bf16[256,384]{1,0:T(8,128)(2,1)} %cent_ref.1), channel_id=1, source_target_pairs={{0,1},{1,0},{2,3},{3,2},{4,5},{5,4},{6,7},{7,6},{8,9},{9,8},{10,11... | collective-permute-start | bytes 589832 | tf_op jit(solution)/shard_map/ppermute | solution.py:165
  4.2 0.7 %copy-start = (bf16[256,384]{1,0:T(8,128)(2,1)}, bf16[256,384]{1,0:T(8,128)(2,1)S(1)}, u32[]{:S(2)}) copy-start(bf16[256,384]{1,0:T(8,128)(2,1)S(1)} %collective-permute-done.other_ref) | copy-start | bytes 589828

commit v3 on v2

--- a/solution.py
+++ b/solution.py
@@ -14,6 +14,10 @@
 
 
 VMEM = pl.BlockSpec(memory_space=pltpu.VMEM)
+
+
+def on_chip(array):
+    return pltpu.with_memory_space_constraint(array, pltpu.VMEM)
 
 
 def iota_f32(shape, axis):
@@ -162,13 +166,14 @@
     width = own * sub_width
     features = vectors.shape[1]
     total = subspaces * sides
-    other = lax.ppermute(centroids, "gy", [(0, 1), (1, 0)])
+    other = on_chip(lax.ppermute(centroids, "gy", [(0, 1), (1, 0)]))
+    rotation = on_chip(rotation)
     turned, digits, code = pl.pallas_call(
         functools.partial(prepare_kernel, own),
         out_shape=(
-            jax.ShapeDtypeStruct((features, LANES), BF16),
-            jax.ShapeDtypeStruct((8, LANES), BF16),
-            jax.ShapeDtypeStruct((own * codes, width + 8), BF16),
+            pltpu.VMEM((features, LANES), BF16),
+            pltpu.VMEM((8, LANES), BF16),
+            pltpu.VMEM((own * codes, width + 8), BF16),
         ),
         in_specs=[VMEM] * 6,
         out_specs=(VMEM, VMEM, VMEM),
@@ -183,15 +188,15 @@
     )
     outgoing = pl.pallas_call(
         functools.partial(pack_kernel, width),
-        out_shape=jax.ShapeDtypeStruct((devices, 2 * width + 8, LANES), BF16),
+        out_shape=pltpu.VMEM((devices, 2 * width + 8, LANES), BF16),
         in_specs=[VMEM] * 5,
         out_specs=VMEM,
         name="pack",
-    )(centroids, other, rotation, turned, digits)
+    )(on_chip(centroids), other, rotation, on_chip(turned), on_chip(digits))
     incoming = lax.all_to_all(outgoing, ("gx", "gy"), split_axis=0, concat_axis=0, tiled=True)
     returning = pl.pallas_call(
         functools.partial(encode_kernel, own, sub_width),
-        out_shape=jax.ShapeDtypeStruct((devices, 16, LANES), BF16),
+        out_shape=pltpu.VMEM((devices, 16, LANES), BF16),
         scratch_shapes=[
             pltpu.VMEM((owners * width, WIDE), F32),
             pltpu.VMEM((width + 8, devices * LANES), BF16),
@@ -200,7 +205,7 @@
         in_specs=[VMEM] * 2,
         out_specs=VMEM,
         name="encode",
-    )(incoming, code)
+    )(on_chip(incoming), on_chip(code))
     returned = lax.all_to_all(returning, ("gx", "gy"), split_axis=0, concat_axis=0, tiled=True)
     quant_error, list_error = pl.pallas_call(
         functools.partial(finish_kernel, own),
@@ -211,7 +216,7 @@
         in_specs=[VMEM],
         out_specs=(VMEM, VMEM),
         name="finish",
-    )(returned)
+    )(on_chip(returned))
     return quant_error.T, list_error.T
 
 

time: 48.2 us -> 41.8 us (0.87)
  Pallas kernels: 13.1 us -> 7.1 us
  blocking collectives: 32.9 us -> 32 us
  local copies, waits for them, and re-layouts: 0.67 us -> 1.27 us
    pallas_call x2, Pallas kernels: 5.76 us -> 2.4 us  [the longest x1 1.93 us: on_device_by_column(): pl.pallas_call(functools.partial(prepare_kernel, own), out_shape=(pltpu.V...]
    pallas_call x1, Pallas kernels: 5.77 us -> 4.06 us  [on_device_by_column(): pl.pallas_call(functools.partial(encode_kernel, own, sub_width), out_shap...]
    pallas_call x1, Pallas kernels: 1.55 us -> 0.65 us  [on_device_by_column(): pl.pallas_call(functools.partial(finish_kernel, own), out_shape=(jax.Shap...]
    all_to_all x1, blocking collectives: 11.4 us -> 10.8 us  [on_device_by_column(): lax.all_to_all(returning, ('gx', 'gy'), split_axis=0, concat_axis=0, tile...]
    unnamed x2 -> x4, local copies, waits for them, and re-layouts: 0.67 us -> 1.27 us
  transfers between devices with their start and end apart: 1 -> 1, of which waited for: 0 -> 0; matrix products, arithmetic and copies ran while one was open for 0% -> 0% of each run, Pallas kernels for 6% -> 5%
where the time goes in v3:
time: 41.8 us; the launch traced here: 41.6 us
  blocking collectives  32 us (77%)
  Pallas kernels  7.1 us (17%)
  local copies, waits for them, and re-layouts  1.27 us (3%)
  between operations  0.67 us (2%)
  starting transfers between devices  0.56 us (1%)
    all_to_all x1, blocking collectives, on_device_by_column(): lax.all_to_all(outgoing, ('gx', 'gy'), split_axis=0, concat_axis=0, tiled...  21.2 us
    all_to_all x1, blocking collectives, on_device_by_column(): lax.all_to_all(returning, ('gx', 'gy'), split_axis=0, concat_axis=0, tile...  10.8 us
    pallas_call x1, Pallas kernels, on_device_by_column(): pl.pallas_call(functools.partial(encode_kernel, own, sub_width), out_shap...  4.06 us
    pallas_call x1, Pallas kernels, on_device_by_column(): pl.pallas_call(functools.partial(prepare_kernel, own), out_shape=(pltpu.V...  1.93 us
    unnamed x4, local copies, waits for them, and re-layouts  1.27 us
  transfers between devices with their start and end apart: 1, of which 0 were waited for; matrix products, arithmetic and copies ran while one was open for 0% of the time, Pallas kernels for 5%

profile of v3, /device:TPU:0, one launch (start us, length us, event | category | flops | bytes accessed | tf_op | source)
XLA Modules:
  0.0 41.6 jit_solution(2657621627918155288)
XLA Ops:
  0.6 0.6 %collective-permute-start = (bf16[256,384]{1,0:T(8,128)(2,1)}, bf16[256,384]{1,0:T(8,128)(2,1)S(1)}, u32[]{:S(2)}, u32[]{:S(2)}) collective-permute-start(bf16[256,384]{1,0:T(8,128)(2,1)} %cent_ref.1), channel_id=1, source_target_pairs={{0,1},{1,0},{2,3},{3,2},{4,5},{5,4},{6,7},{7,6},{8,9},{9,8},{10,11... | collective-permute-start | bytes 589832 | tf_op jit(solution)/shard_map/ppermute | solution.py:169
  1.2 0.0 copy-start
  1.2 1.3 %copy-done = bf16[768,768]{1,0:T(8,128)(2,1)S(1)} copy-done((bf16[768,768]{1,0:T(8,128)(2,1)S(1)}, bf16[768,768]{1,0:T(8,128)(2,1)}, u32[]{:S(2)}) %copy-start) | copy-done | bytes 1179672
  2.5 0.0 copy-start.1
  2.5 1.9 %prepare.1 = (bf16[768,128]{1,0:T(8,128)(2,1)S(1)}, bf16[8,128]{1,0:T(8,128)(2,1)S(1)}, bf16[768,32]{1,0:T(8,128)(2,1)S(1)}) custom-call(s32[1,128]{1,0:T(1,128)} %bitcast.7, s32[32,128]{1,0:T(8,128)} %bitcast.5, s32[32,128]{1,0:T(8,128)} %bitcast.6, bf16[128,768]{1,0:T(8,128)(2,1)} %vec_ref.1, bf16[768,768]{1,0:T(8,128)(2,1)S(1)} %copy-done, ...), custom_call_target="tpu_custom_call" | custom-call | tf_op jit(solution)/shard_map/prepare/pallas_call | solution.py:171
  4.4 0.0 collective-permute-done.other_ref
  4.4 0.0 copy-done.1
  4.4 0.5 %pack.1 = bf16[32,56,128]{2,1,0:T(8,128)(2,1)S(1)} custom-call(bf16[256,384]{1,0:T(8,128)(2,1)S(1)} %copy-done.1, bf16[256,384]{1,0:T(8,128)(2,1)S(1)} %collective-permute-done.other_ref, bf16[768,768]{1,0:T(8,128)(2,1)S(1)} %copy-done, bf16[768,128]{1,0:T(8,128)(2,1)S(1)} %get-tuple-element.7.turned_ref, bf16[8,128]{1,0:T(8,128)(2,1)S(1)} %get-tuple-element.8.digit_ref), custom_call_target="tpu_custom_call" | custom-call | tf_op jit(solution)/shard_map/pack/pallas_call | solution.py:189
  4.9 21.2 %all_to_all.10.in_ref = bf16[32,56,128]{2,1,0:T(8,128)(2,1)S(1)} all-to-all(bf16[32,56,128]{2,1,0:T(8,128)(2,1)S(1)} %pack.1), channel_id=1, replica_groups=mesh['gx'=16,'gy'=2] {'gx','gy'}, dimensions={0} | all-to-all | bytes 917504 | tf_op jit(solution)/shard_map/all_to_all | solution.py:196
  26.1 4.1 %encode.1 = bf16[32,16,128]{2,1,0:T(8,128)(2,1)S(1)} custom-call(bf16[32,56,128]{2,1,0:T(8,128)(2,1)S(1)} %all_to_all.10.in_ref, bf16[768,32]{1,0:T(8,128)(2,1)S(1)} %get-tuple-element.9.code_ref), custom_call_target="tpu_custom_call" | custom-call | tf_op jit(solution)/shard_map/encode/pallas_call | solution.py:197
  30.1 10.8 %all_to_all.11.in_ref = bf16[32,16,128]{2,1,0:T(8,128)(2,1)S(1)} all-to-all(bf16[32,16,128]{2,1,0:T(8,128)(2,1)S(1)} %encode.1), channel_id=1, replica_groups=mesh['gx'=16,'gy'=2] {'gx','gy'}, dimensions={0} | all-to-all | bytes 262144 | tf_op jit(solution)/shard_map/all_to_all | solution.py:209
  40.9 0.6 %finish.1 = (f32[96,128]{1,0:T(8,128)}, f32[48,256]{1,0:T(8,128)}) custom-call(bf16[32,16,128]{2,1,0:T(8,128)(2,1)S(1)} %all_to_all.11.in_ref), custom_call_target="tpu_custom_call" | custom-call | tf_op jit(solution)/shard_map/finish/pallas_call | solution.py:210
Async XLA Ops:
  0.6 3.8 %collective-permute-start = (bf16[256,384]{1,0:T(8,128)(2,1)}, bf16[256,384]{1,0:T(8,128)(2,1)S(1)}, u32[]{:S(2)}, u32[]{:S(2)}) collective-permute-start(bf16[256,384]{1,0:T(8,128)(2,1)} %cent_ref.1), channel_id=1, source_target_pairs={{0,1},{1,0},{2,3},{3,2},{4,5},{5,4},{6,7},{7,6},{8,9},{9,8},{10,11... | collective-permute-start | bytes 589832 | tf_op jit(solution)/shard_map/ppermute | solution.py:169
  1.2 1.3 %copy-start = (bf16[768,768]{1,0:T(8,128)(2,1)S(1)}, bf16[768,768]{1,0:T(8,128)(2,1)}, u32[]{:S(2)}) copy-start(bf16[768,768]{1,0:T(8,128)(2,1)} %rot_ref.3) | copy-start | bytes 3538948
  2.5 1.9 %copy-start.1 = (bf16[256,384]{1,0:T(8,128)(2,1)S(1)}, bf16[256,384]{1,0:T(8,128)(2,1)}, u32[]{:S(2)}) copy-start(bf16[256,384]{1,0:T(8,128)(2,1)} %cent_ref.1) | copy-start | bytes 589828

commit v4 on v3

--- a/solution.py
+++ b/solution.py
@@ -41,20 +41,38 @@
     return high, slot - high * WIDE
 
 
-def prepare_kernel(own, ids_ref, old_ref, new_ref, vec_ref, rot_ref, book_ref, turned_ref, digit_ref, code_ref):
+def prepare_kernel(
+    own, ids_hbm, old_hbm, new_hbm, book_hbm, vec_hbm, rot_hbm, cent_hbm,
+    turned_ref, digit_ref, code_ref, rot_ref, mine_ref, ids_ref, old_ref, new_ref, book_ref, vec_ref, arrived,
+):
+    first = lax.axis_index("gx") * own
+    side = lax.axis_index("gy")
+    moves = (
+        (ids_hbm, ids_ref),
+        (old_hbm, old_ref),
+        (new_hbm, new_ref),
+        (book_hbm.at[pl.ds(first, own)], book_ref),
+        (vec_hbm, vec_ref),
+        (rot_hbm, rot_ref),
+        (cent_hbm.at[pl.ds(side * LANES, LANES)], mine_ref),
+    )
+    copies = [pltpu.make_async_copy(src, dst, arrived.at[n]) for n, (src, dst) in enumerate(moves)]
+    for copy in copies:
+        copy.start()
+    for copy in copies[:3]:
+        copy.wait()
     ids_across = jnp.broadcast_to(ids_ref[...], (LANES, LANES)).astype(F32).T.astype(jnp.int32)
     old_high, old_low = slot_digits(ids_across, old_ref)
     new_high, new_low = slot_digits(ids_across, new_ref)
     row = lax.broadcasted_iota(jnp.int32, (8, LANES), 0)
     digits = jnp.where(row == 0, old_high, jnp.where(row == 1, old_low, jnp.where(row == 2, new_high, new_low)))
     digit_ref[...] = digits.astype(BF16)
-    turned_ref[...] = dot(vec_ref[...], rot_ref[...]).T.astype(BF16)
+    copies[3].wait()
     codes = book_ref.shape[2]
-    first = lax.axis_index("gx") * own
     row = lax.broadcasted_iota(jnp.int32, (8, codes), 0)
     parts, tails = [], []
     for m in range(own):
-        words = book_ref[first + m].astype(F32)
+        words = book_ref[m].astype(F32)
         zero = jnp.zeros_like(words)
         parts.append(jnp.concatenate([-2.0 * words if n == m else zero for n in range(own)], axis=1))
         norm = jnp.sum(words * words, axis=0, keepdims=True)
@@ -64,22 +82,28 @@
         tails.append(jnp.where(row == 0, top, jnp.where(row == 1, middle, jnp.where(row == 2, low, 0.0))))
     parts.append(jnp.concatenate(tails, axis=1))
     code_ref[...] = jnp.concatenate(parts, axis=0).T.astype(BF16)
-
-
-def pack_kernel(width, cent_ref, other_ref, rot_ref, turned_ref, digit_ref, out_ref):
+    copies[4].wait()
+    copies[5].wait()
+    turned_ref[...] = dot(vec_ref[...], rot_ref[...]).T.astype(BF16)
+    copies[6].wait()
+
+
+def pack_kernel(width, mine_ref, other_ref, rot_ref, turned_ref, digit_ref, out_ref):
     side = lax.axis_index("gy")
-    half = cent_ref.shape[1]
-    mine = cent_ref[pl.ds(side * LANES, LANES), :]
+    half = mine_ref.shape[1]
     other = other_ref[pl.ds(side * LANES, LANES), :]
-    rotated = dot(mine, rot_ref[pl.ds(side * half, half), :])
+    rotated = dot(mine_ref[...], rot_ref[pl.ds(side * half, half), :])
     rotated += dot(other, rot_ref[pl.ds((1 - side) * half, half), :])
     cents = rotated.T
     vectors = turned_ref[...].astype(F32)
     digits = digit_ref[...].astype(F32)
     for device in range(out_ref.shape[0]):
         at = (device % 2) * half + (device // 2) * width
-        block = jnp.concatenate([vectors[at : at + width], cents[at : at + width], digits], axis=0)
-        out_ref[device] = block.astype(BF16)
+        for part in range(width // 4):
+            rows = slice(at + 4 * part, at + 4 * part + 4)
+            out_ref[device, part] = vectors[rows].astype(BF16)
+            out_ref[device, width // 4 + part] = cents[rows].astype(BF16)
+        out_ref[device, width // 2] = digits[0:4].astype(BF16)
 
 
 def encode_kernel(own, sub_width, in_ref, code_ref, out_ref, table_ref, low_ref, square_ref):
@@ -89,9 +113,12 @@
     codes = code_ref.shape[0] // own
 
     def pair(tile, lo, hi):
-        return jnp.concatenate([in_ref[2 * tile, lo:hi, :], in_ref[2 * tile + 1, lo:hi, :]], axis=1).astype(F32)
-
-    digits = [pair(tile, 2 * width, 2 * width + 8) for tile in range(tiles)]
+        rows = []
+        for part in range(lo // 4, hi // 4):
+            rows.append(jnp.concatenate([in_ref[2 * tile, part], in_ref[2 * tile + 1, part]], axis=1).astype(F32))
+        return jnp.concatenate(rows, axis=0) if len(rows) > 1 else rows[0]
+
+    digits = [pair(tile, 2 * width, 2 * width + 4) for tile in range(tiles)]
     for tile in range(tiles):
         table_ref[tile * width : (tile + 1) * width, :] = pair(tile, width, 2 * width)
     table = table_ref[...].astype(BF16)
@@ -138,12 +165,11 @@
         group = sums[tile * 8 : (tile + 1) * 8]
         total = group[0:own] + group[own : 2 * own]
         mean = total / jnp.maximum(group[2 * own : 2 * own + 1], 1.0)
-        pad = jnp.zeros((out_ref.shape[1] - 3 * own, LANES), F32)
+        pad = jnp.zeros((out_ref.shape[2] - own, LANES), F32)
         for side in range(2):
-            block = jnp.concatenate(
-                [errors[tile][:, side * LANES : (side + 1) * LANES], mean[:, :LANES], mean[:, LANES:], pad], axis=0
-            )
-            out_ref[2 * tile + side] = block.astype(BF16)
+            error = errors[tile][:, side * LANES : (side + 1) * LANES]
+            for part, rows in enumerate((error, mean[:, :LANES], mean[:, LANES:])):
+                out_ref[2 * tile + side, part] = jnp.concatenate([rows, pad], axis=0).astype(BF16)
 
 
 def finish_kernel(own, in_ref, quant_ref, list_ref):
@@ -151,11 +177,11 @@
     side = lax.axis_index("gy")
     for device in range(2 * tiles):
         at = ((device % 2) * tiles + device // 2) * own
-        quant_ref[at : at + own, :] = in_ref[device].astype(F32)[0:own]
-    for tile in range(tiles):
-        block = in_ref[2 * tile + side].astype(F32)
-        list_ref[tile * own : (tile + 1) * own, 0:LANES] = block[own : 2 * own]
-        list_ref[tile * own : (tile + 1) * own, LANES:WIDE] = block[2 * own : 3 * own]
+        quant_ref[at : at + own, :] = in_ref[device, 0].astype(F32)[0:own]
+    for tile in range(tiles):
+        at = tile * own
+        list_ref[at : at + own, 0:LANES] = in_ref[2 * tile + side, 1].astype(F32)[0:own]
+        list_ref[at : at + own, LANES:WIDE] = in_ref[2 * tile + side, 2].astype(F32)[0:own]
 
 
 def on_device_by_column(vectors, list_ids, old_order, new_order, centroids, rotation, codebook):
@@ -166,37 +192,47 @@
     width = own * sub_width
     features = vectors.shape[1]
     total = subspaces * sides
-    other = on_chip(lax.ppermute(centroids, "gy", [(0, 1), (1, 0)]))
-    rotation = on_chip(rotation)
-    turned, digits, code = pl.pallas_call(
+    other = lax.ppermute(centroids, "gy", [(0, 1), (1, 0)])
+    turned, digits, code, rotation, mine = pl.pallas_call(
         functools.partial(prepare_kernel, own),
         out_shape=(
             pltpu.VMEM((features, LANES), BF16),
             pltpu.VMEM((8, LANES), BF16),
             pltpu.VMEM((own * codes, width + 8), BF16),
+            pltpu.VMEM(rotation.shape, BF16),
+            pltpu.VMEM((LANES, centroids.shape[1]), BF16),
         ),
-        in_specs=[VMEM] * 6,
-        out_specs=(VMEM, VMEM, VMEM),
+        in_specs=[pl.BlockSpec(memory_space=pl.ANY)] * 7,
+        out_specs=(VMEM,) * 5,
+        scratch_shapes=[
+            pltpu.VMEM((1, LANES), jnp.int32),
+            pltpu.VMEM((old_order.shape[0] // LANES, LANES), jnp.int32),
+            pltpu.VMEM((old_order.shape[0] // LANES, LANES), jnp.int32),
+            pltpu.VMEM((own, sub_width, codes), BF16),
+            pltpu.VMEM((LANES, features), BF16),
+            pltpu.SemaphoreType.DMA((7,)),
+        ],
         name="prepare",
     )(
         list_ids.reshape(1, LANES),
         old_order.reshape(-1, LANES),
         new_order.reshape(-1, LANES),
+        codebook,
         vectors,
         rotation,
-        codebook,
+        centroids,
     )
     outgoing = pl.pallas_call(
         functools.partial(pack_kernel, width),
-        out_shape=pltpu.VMEM((devices, 2 * width + 8, LANES), BF16),
+        out_shape=pltpu.VMEM((devices, width // 2 + 1, 4, LANES), BF16),
         in_specs=[VMEM] * 5,
         out_specs=VMEM,
         name="pack",
-    )(on_chip(centroids), other, rotation, on_chip(turned), on_chip(digits))
+    )(*(on_chip(array) for array in (mine, other, rotation, turned, digits)))
     incoming = lax.all_to_all(outgoing, ("gx", "gy"), split_axis=0, concat_axis=0, tiled=True)
     returning = pl.pallas_call(
         functools.partial(encode_kernel, own, sub_width),
-        out_shape=pltpu.VMEM((devices, 16, LANES), BF16),
+        out_shape=pltpu.VMEM((devices, 3, 4, LANES), BF16),
         scratch_shapes=[
             pltpu.VMEM((owners * width, WIDE), F32),
             pltpu.VMEM((width + 8, devices * LANES), BF16),

time: 41.8 us -> 39.4 us (0.943)
  local copies, waits for them, and re-layouts: 1.27 us -> 0 us
  blocking collectives: 32 us -> 30.8 us
    unnamed x4 -> x0, local copies, waits for them, and re-layouts: 1.27 us -> none
    all_to_all x1, blocking collectives: 21.2 us -> 20.6 us  [on_device_by_column(): lax.all_to_all(outgoing, ('gx', 'gy'), split_axis=0, concat_axis=0, tiled...]
    all_to_all x1, blocking collectives: 10.8 us -> 10.2 us  [on_device_by_column(): lax.all_to_all(returning, ('gx', 'gy'), split_axis=0, concat_axis=0, tile...]
where the time goes in v4:
time: 39.4 us; the launch traced here: 39.2 us
  blocking collectives  30.8 us (78%)
  Pallas kernels  7.18 us (18%)
  between operations  0.66 us (2%)
  starting transfers between devices  0.56 us (1%)
    all_to_all x1, blocking collectives, on_device_by_column(): lax.all_to_all(outgoing, ('gx', 'gy'), split_axis=0, concat_axis=0, tiled...  20.6 us
    all_to_all x1, blocking collectives, on_device_by_column(): lax.all_to_all(returning, ('gx', 'gy'), split_axis=0, concat_axis=0, tile...  10.2 us
    pallas_call x1, Pallas kernels, on_device_by_column(): pl.pallas_call(functools.partial(encode_kernel, own, sub_width), out_shap...  4.05 us
    pallas_call x1, Pallas kernels, on_device_by_column(): pl.pallas_call(functools.partial(prepare_kernel, own), out_shape=(pltpu.V...  1.98 us
  transfers between devices with their start and end apart: 1, of which 0 were waited for; matrix products, arithmetic and copies ran while one was open for 0% of the time, Pallas kernels for 5%

profile of v4, /device:TPU:0, one launch (start us, length us, event | category | flops | bytes accessed | tf_op | source)
XLA Modules:
  0.0 39.2 jit_solution(15236210944022176882)
XLA Ops:
  0.6 0.6 %collective-permute-start = (bf16[256,384]{1,0:T(8,128)(2,1)}, bf16[256,384]{1,0:T(8,128)(2,1)S(1)}, u32[]{:S(2)}, u32[]{:S(2)}) collective-permute-start(bf16[256,384]{1,0:T(8,128)(2,1)} %cent_hbm.1), channel_id=1, source_target_pairs={{0,1},{1,0},{2,3},{3,2},{4,5},{5,4},{6,7},{7,6},{8,9},{9,8},{10,11... | collective-permute-start | bytes 589832 | tf_op jit(solution)/shard_map/ppermute | solution.py:195
  1.2 2.0 %prepare.1 = (bf16[768,128]{1,0:T(8,128)(2,1)S(1)}, bf16[8,128]{1,0:T(8,128)(2,1)S(1)}, bf16[768,32]{1,0:T(8,128)(2,1)S(1)}, bf16[768,768]{1,0:T(8,128)(2,1)S(1)}, bf16[128,384]{1,0:T(8,128)(2,1)S(1)}) custom-call(s32[1,128]{1,0:T(1,128)} %bitcast.7, s32[32,128]{1,0:T(8,128)} %bitcast.5, s32[32,128]{1,0:T(8,128)} %bitcast.6, bf16[48,8,256]{2,1,0:T(8,128)(2,1)} %book_hbm.1, ...), custom_call_target="tpu_custom_call" | custom-call | tf_op jit(solution)/shard_map/prepare/pallas_call | solution.py:196
  3.2 0.0 collective-permute-done.other_ref
  3.2 0.5 %pack.1 = bf16[32,13,4,128]{3,2,1,0:T(4,128)(2,1)S(1)} custom-call(bf16[128,384]{1,0:T(8,128)(2,1)S(1)} %get-tuple-element.9.mine_ref, bf16[256,384]{1,0:T(8,128)(2,1)S(1)} %collective-permute-done.other_ref, bf16[768,768]{1,0:T(8,128)(2,1)S(1)} %get-tuple-element.10.rot_ref, bf16[768,128]{1,0:T(8,128)(2,1)S(1)} %get-tuple-element.11.turned_ref, ...), custom_call_target="tpu_custom_call" | custom-call | tf_op jit(solution)/shard_map/pack/pallas_call | solution.py:225
  3.7 20.6 %all_to_all.10.in_ref = bf16[32,13,4,128]{3,2,1,0:T(4,128)(2,1)S(1)} all-to-all(bf16[32,13,4,128]{3,2,1,0:T(4,128)(2,1)S(1)} %pack.1), channel_id=1, replica_groups=mesh['gx'=16,'gy'=2] {'gx','gy'}, dimensions={0} | all-to-all | bytes 851968 | tf_op jit(solution)/shard_map/all_to_all | solution.py:232
  24.3 4.0 %encode.1 = bf16[32,3,4,128]{3,2,1,0:T(4,128)(2,1)S(1)} custom-call(bf16[32,13,4,128]{3,2,1,0:T(4,128)(2,1)S(1)} %all_to_all.10.in_ref, bf16[768,32]{1,0:T(8,128)(2,1)S(1)} %get-tuple-element.13.code_ref), custom_call_target="tpu_custom_call" | custom-call | tf_op jit(solution)/shard_map/encode/pallas_call | solution.py:233
  28.3 10.2 %all_to_all.11.in_ref = bf16[32,3,4,128]{3,2,1,0:T(4,128)(2,1)S(1)} all-to-all(bf16[32,3,4,128]{3,2,1,0:T(4,128)(2,1)S(1)} %encode.1), channel_id=1, replica_groups=mesh['gx'=16,'gy'=2] {'gx','gy'}, dimensions={0} | all-to-all | bytes 196608 | tf_op jit(solution)/shard_map/all_to_all | solution.py:245
  38.6 0.6 %finish.1 = (f32[96,128]{1,0:T(8,128)}, f32[48,256]{1,0:T(8,128)}) custom-call(bf16[32,3,4,128]{3,2,1,0:T(4,128)(2,1)S(1)} %all_to_all.11.in_ref), custom_call_target="tpu_custom_call" | custom-call | tf_op jit(solution)/shard_map/finish/pallas_call | solution.py:246
Async XLA Ops:
  0.6 2.5 %collective-permute-start = (bf16[256,384]{1,0:T(8,128)(2,1)}, bf16[256,384]{1,0:T(8,128)(2,1)S(1)}, u32[]{:S(2)}, u32[]{:S(2)}) collective-permute-start(bf16[256,384]{1,0:T(8,128)(2,1)} %cent_hbm.1), channel_id=1, source_target_pairs={{0,1},{1,0},{2,3},{3,2},{4,5},{5,4},{6,7},{7,6},{8,9},{9,8},{10,11... | collective-permute-start | bytes 589832 | tf_op jit(solution)/shard_map/ppermute | solution.py:195

commit v5 on v4

--- a/solution.py
+++ b/solution.py
@@ -26,6 +26,19 @@
 
 def dot(a, b, contract=((1,), (0,))):
     return lax.dot_general(a, b, (contract, ((), ())), preferred_element_type=F32)
+
+
+def pick_lanes(rows, index):
+    along = lax.GatherDimensionNumbers(
+        offset_dims=(),
+        collapsed_slice_dims=(1,),
+        start_index_map=(1,),
+        operand_batching_dims=(0,),
+        start_indices_batching_dims=(0,),
+    )
+    return lax.gather(
+        rows, index[..., None], along, slice_sizes=(1, 1), mode=lax.GatherScatterMode.PROMISE_IN_BOUNDS
+    )
 
 
 def slot_digits(ids_across, order_ref):
@@ -106,70 +119,83 @@
         out_ref[device, width // 2] = digits[0:4].astype(BF16)
 
 
-def encode_kernel(own, sub_width, in_ref, code_ref, out_ref, table_ref, low_ref, square_ref):
+def encode_kernel(own, sub_width, in_ref, code_ref, out_ref, table_ref, low_ref):
     devices = in_ref.shape[0]
     tiles = devices // 2
     width = own * sub_width
+    parts = width // 4
     codes = code_ref.shape[0] // own
 
-    def pair(tile, lo, hi):
-        rows = []
-        for part in range(lo // 4, hi // 4):
-            rows.append(jnp.concatenate([in_ref[2 * tile, part], in_ref[2 * tile + 1, part]], axis=1).astype(F32))
-        return jnp.concatenate(rows, axis=0) if len(rows) > 1 else rows[0]
-
-    digits = [pair(tile, 2 * width, 2 * width + 4) for tile in range(tiles)]
+    def stack(device, first):
+        return jnp.concatenate([in_ref[device, first + n].astype(F32) for n in range(parts)], axis=0)
+
+    digits = [in_ref[device, 2 * parts].astype(F32) for device in range(devices)]
     for tile in range(tiles):
-        table_ref[tile * width : (tile + 1) * width, :] = pair(tile, width, 2 * width)
-    table = table_ref[...].astype(BF16)
-    sub = iota_f32((WIDE, WIDE), 0)
-    tail_row = lax.broadcasted_iota(jnp.int32, (8, WIDE), 0)
-    tail = (tail_row < 3).astype(F32)
-    for tile in range(tiles):
-        hot = (sub == digits[tile][1:2]).astype(F32).astype(BF16)
-        looked = dot(table, hot)
-        high = jnp.broadcast_to(digits[tile][0:1], (width, WIDE))
-        cent = jnp.zeros((width, WIDE), F32)
-        for group in range(tiles):
-            cent = jnp.where(high == float(group), looked[group * width : (group + 1) * width], cent)
-        turned = pair(tile, 0, width) - cent
-        lanes = slice(tile * WIDE, (tile + 1) * WIDE)
-        low_ref[:, lanes] = jnp.concatenate([turned, tail], axis=0).astype(BF16)
+        rows = jnp.concatenate([stack(2 * tile, parts), stack(2 * tile + 1, parts)], axis=0)
+        table_ref[tile] = rows.astype(BF16)
+    lane = lax.broadcasted_iota(jnp.int32, (WIDE, WIDE), 0).astype(F32)
+    tail = (lax.broadcasted_iota(jnp.int32, (8, LANES), 0) < 3).astype(F32)
+    code = code_ref[...]
+
+    def turn(device):
+        chunks = 2 * width // 16
+        group = jnp.broadcast_to(digits[device][0:1], (16, LANES)).astype(BF16)
+        place = digits[device][1:2]
+        odd = place >= float(LANES)
+        index = jnp.where(odd, place - float(LANES), place).astype(jnp.int32)
+        index = jnp.broadcast_to(index, (16, LANES)).astype(jnp.int16)
+        found = [jnp.zeros((16, LANES), BF16) for _ in range(chunks)]
+        for tile in range(tiles):
+            here = group == jnp.asarray(tile, BF16)
+            for n in range(chunks):
+                found[n] = jnp.where(here, pick_lanes(table_ref[tile, 16 * n : 16 * n + 16, :], index), found[n])
+        both = jnp.concatenate([part.astype(F32) for part in found], axis=0)
+        odd = jnp.broadcast_to(odd, (width, LANES))
+        turned = stack(device, 0) - jnp.where(odd, both[width:], both[:width])
+        low_ref[device] = jnp.concatenate([turned, tail], axis=0).astype(BF16)
         squared = turned * turned
-        for m in range(own):
-            square_ref[m : m + 1, lanes] = jnp.sum(
-                squared[m * sub_width : (m + 1) * sub_width], axis=0, keepdims=True
-            )
-    code = code_ref[...]
+        return jnp.concatenate(
+            [jnp.sum(squared[8 * n : 8 * n + 8], axis=0, keepdims=True) for n in range(own)], axis=0
+        )
+
+    def measure(tile, squares):
+        low = jnp.concatenate([low_ref[2 * tile], low_ref[2 * tile + 1]], axis=1)
+        distance = dot(code, low)
+        nearest = [jnp.min(distance[m * codes : (m + 1) * codes], axis=0, keepdims=True) for m in range(own)]
+        return jnp.concatenate(nearest, axis=0) + jnp.concatenate(squares, axis=1)
+
+    def gather(tile, error, sums):
+        pair = jnp.concatenate([digits[2 * tile], digits[2 * tile + 1]], axis=1)
+        top = error.astype(BF16).astype(F32)
+        pad = jnp.zeros((8 - 2 * own - 1, WIDE), F32)
+        for side in range(2):
+            out_ref[2 * tile + side, 0] = jnp.concatenate([top, error - top], axis=0)[
+                0:4, side * LANES : (side + 1) * LANES
+            ].astype(BF16)
+        rows = jnp.concatenate([top, error - top, jnp.ones((1, WIDE), F32), pad], axis=0)
+        high = jnp.broadcast_to(pair[2:3], (8, WIDE))
+        spread = jnp.concatenate([jnp.where(high == float(group), rows, 0.0) for group in range(tiles)], axis=0)
+        hot = (pair[3:4] == lane).astype(F32).astype(BF16)
+        return sums + dot(spread.astype(BF16), hot, ((1,), (1,)))
+
     sums = jnp.zeros((tiles * 8, WIDE), F32)
     errors = []
+    squares = [turn(0), turn(1)]
     for tile in range(tiles):
-        lanes = slice(tile * WIDE, (tile + 1) * WIDE)
-        distance = dot(code, low_ref[:, lanes])
-        nearest = jnp.concatenate(
-            [jnp.min(distance[m * codes : (m + 1) * codes], axis=0, keepdims=True) for m in range(own)], axis=0
-        )
-        error = nearest + square_ref[0:own, lanes]
-        errors.append(error)
-        top = error.astype(BF16).astype(F32)
-        rest = error - top
-        pad = jnp.zeros((8 - 2 * own - 1, WIDE), F32)
-        group_rows = jnp.concatenate([top, rest, jnp.ones((1, WIDE), F32), pad], axis=0)
-        high = jnp.broadcast_to(digits[tile][2:3], (8, WIDE))
-        spread = jnp.concatenate(
-            [jnp.where(high == float(group), group_rows, 0.0) for group in range(tiles)], axis=0
-        ).astype(BF16)
-        hot = (sub == digits[tile][3:4]).astype(F32).astype(BF16)
-        sums = sums + dot(spread, hot, ((1,), (1,)))
+        ahead = [turn(2 * tile + 2), turn(2 * tile + 3)] if tile + 1 < tiles else None
+        errors.append(measure(tile, squares))
+        if tile:
+            sums = gather(tile - 1, errors[tile - 1], sums)
+        squares = ahead
+    sums = gather(tiles - 1, errors[tiles - 1], sums)
     for tile in range(tiles):
         group = sums[tile * 8 : (tile + 1) * 8]
         total = group[0:own] + group[own : 2 * own]
         mean = total / jnp.maximum(group[2 * own : 2 * own + 1], 1.0)
         pad = jnp.zeros((out_ref.shape[2] - own, LANES), F32)
         for side in range(2):
-            error = errors[tile][:, side * LANES : (side + 1) * LANES]
-            for part, rows in enumerate((error, mean[:, :LANES], mean[:, LANES:])):
-                out_ref[2 * tile + side, part] = jnp.concatenate([rows, pad], axis=0).astype(BF16)
+            for part, rows in enumerate((mean[:, :LANES], mean[:, LANES:])):
+                out_ref[2 * tile + side, part + 1] = jnp.concatenate([rows, pad], axis=0).astype(BF16)
 
 
 def finish_kernel(own, in_ref, quant_ref, list_ref):
@@ -234,9 +260,8 @@
         functools.partial(encode_kernel, own, sub_width),
         out_shape=pltpu.VMEM((devices, 3, 4, LANES), BF16),
         scratch_shapes=[
-            pltpu.VMEM((owners * width, WIDE), F32),
-            pltpu.VMEM((width + 8, devices * LANES), BF16),
-            pltpu.VMEM((8, devices * LANES), F32),
+            pltpu.VMEM((owners, 2 * width, LANES), BF16),
+            pltpu.VMEM((devices, width + 8, LANES), BF16),
         ],
         in_specs=[VMEM] * 2,
         out_specs=VMEM,

time: 39.4 us -> 38.4 us (0.975)
  Pallas kernels: 7.18 us -> 6.18 us
    pallas_call x1, Pallas kernels: 4.05 us -> 3.05 us  [on_device_by_column(): pl.pallas_call(functools.partial(encode_kernel, own, sub_width), out_shap...]
where the time goes in v5:
time: 38.4 us; the launch traced here: 38.2 us
  blocking collectives  30.8 us (80%)
  Pallas kernels  6.18 us (16%)
  between operations  0.66 us (2%)
  starting transfers between devices  0.56 us (1%)
    all_to_all x1, blocking collectives, on_device_by_column(): lax.all_to_all(outgoing, ('gx', 'gy'), split_axis=0, concat_axis=0, tiled...  20.6 us
    all_to_all x1, blocking collectives, on_device_by_column(): lax.all_to_all(returning, ('gx', 'gy'), split_axis=0, concat_axis=0, tile...  10.2 us
    pallas_call x1, Pallas kernels, on_device_by_column(): pl.pallas_call(functools.partial(encode_kernel, own, sub_width), out_shap...  3.05 us
    pallas_call x1, Pallas kernels, on_device_by_column(): pl.pallas_call(functools.partial(prepare_kernel, own), out_shape=(pltpu.V...  1.98 us
  transfers between devices with their start and end apart: 1, of which 0 were waited for; matrix products, arithmetic and copies ran while one was open for 0% of the time, Pallas kernels for 5%

profile of v5, /device:TPU:0, one launch (start us, length us, event | category | flops | bytes accessed | tf_op | source)
XLA Modules:
  0.0 38.2 jit_solution(950776440833642167)
XLA Ops:
  0.6 0.6 %collective-permute-start = (bf16[256,384]{1,0:T(8,128)(2,1)}, bf16[256,384]{1,0:T(8,128)(2,1)S(1)}, u32[]{:S(2)}, u32[]{:S(2)}) collective-permute-start(bf16[256,384]{1,0:T(8,128)(2,1)} %cent_hbm.1), channel_id=1, source_target_pairs={{0,1},{1,0},{2,3},{3,2},{4,5},{5,4},{6,7},{7,6},{8,9},{9,8},{10,11... | collective-permute-start | bytes 589832 | tf_op jit(solution)/shard_map/ppermute | solution.py:221
  1.2 2.0 %prepare.1 = (bf16[768,128]{1,0:T(8,128)(2,1)S(1)}, bf16[8,128]{1,0:T(8,128)(2,1)S(1)}, bf16[768,32]{1,0:T(8,128)(2,1)S(1)}, bf16[768,768]{1,0:T(8,128)(2,1)S(1)}, bf16[128,384]{1,0:T(8,128)(2,1)S(1)}) custom-call(s32[1,128]{1,0:T(1,128)} %bitcast.7, s32[32,128]{1,0:T(8,128)} %bitcast.5, s32[32,128]{1,0:T(8,128)} %bitcast.6, bf16[48,8,256]{2,1,0:T(8,128)(2,1)} %book_hbm.1, ...), custom_call_target="tpu_custom_call" | custom-call | tf_op jit(solution)/shard_map/prepare/pallas_call | solution.py:222
  3.2 0.0 collective-permute-done.other_ref
  3.2 0.5 %pack.1 = bf16[32,13,4,128]{3,2,1,0:T(4,128)(2,1)S(1)} custom-call(bf16[128,384]{1,0:T(8,128)(2,1)S(1)} %get-tuple-element.9.mine_ref, bf16[256,384]{1,0:T(8,128)(2,1)S(1)} %collective-permute-done.other_ref, bf16[768,768]{1,0:T(8,128)(2,1)S(1)} %get-tuple-element.10.rot_ref, bf16[768,128]{1,0:T(8,128)(2,1)S(1)} %get-tuple-element.11.turned_ref, ...), custom_call_target="tpu_custom_call" | custom-call | tf_op jit(solution)/shard_map/pack/pallas_call | solution.py:251
  3.7 20.6 %all_to_all.10.in_ref = bf16[32,13,4,128]{3,2,1,0:T(4,128)(2,1)S(1)} all-to-all(bf16[32,13,4,128]{3,2,1,0:T(4,128)(2,1)S(1)} %pack.1), channel_id=1, replica_groups=mesh['gx'=16,'gy'=2] {'gx','gy'}, dimensions={0} | all-to-all | bytes 851968 | tf_op jit(solution)/shard_map/all_to_all | solution.py:258
  24.3 3.1 %encode.1 = bf16[32,3,4,128]{3,2,1,0:T(4,128)(2,1)S(1)} custom-call(bf16[32,13,4,128]{3,2,1,0:T(4,128)(2,1)S(1)} %all_to_all.10.in_ref, bf16[768,32]{1,0:T(8,128)(2,1)S(1)} %get-tuple-element.13.code_ref), custom_call_target="tpu_custom_call" | custom-call | tf_op jit(solution)/shard_map/encode/pallas_call | solution.py:259
  27.3 10.2 %all_to_all.11.in_ref = bf16[32,3,4,128]{3,2,1,0:T(4,128)(2,1)S(1)} all-to-all(bf16[32,3,4,128]{3,2,1,0:T(4,128)(2,1)S(1)} %encode.1), channel_id=1, replica_groups=mesh['gx'=16,'gy'=2] {'gx','gy'}, dimensions={0} | all-to-all | bytes 196608 | tf_op jit(solution)/shard_map/all_to_all | solution.py:270
  37.6 0.6 %finish.1 = (f32[96,128]{1,0:T(8,128)}, f32[48,256]{1,0:T(8,128)}) custom-call(bf16[32,3,4,128]{3,2,1,0:T(4,128)(2,1)S(1)} %all_to_all.11.in_ref), custom_call_target="tpu_custom_call" | custom-call | tf_op jit(solution)/shard_map/finish/pallas_call | solution.py:271
Async XLA Ops:
  0.6 2.5 %collective-permute-start = (bf16[256,384]{1,0:T(8,128)(2,1)}, bf16[256,384]{1,0:T(8,128)(2,1)S(1)}, u32[]{:S(2)}, u32[]{:S(2)}) collective-permute-start(bf16[256,384]{1,0:T(8,128)(2,1)} %cent_hbm.1), channel_id=1, source_target_pairs={{0,1},{1,0},{2,3},{3,2},{4,5},{5,4},{6,7},{7,6},{8,9},{9,8},{10,11... | collective-permute-start | bytes 589832 | tf_op jit(solution)/shard_map/ppermute | solution.py:221

commit v6 on v5

--- a/solution.py
+++ b/solution.py
@@ -42,9 +42,11 @@
 
 
 def slot_digits(ids_across, order_ref):
-    found = jnp.zeros((LANES, LANES), F32)
+    order = order_ref[...].astype(jnp.int16)
+    found = jnp.zeros((LANES, LANES), BF16)
     for block in range(order_ref.shape[0]):
-        found = jnp.where(ids_across == order_ref[block : block + 1, :], float(block + 1), found)
+        found = jnp.where(ids_across == order[block : block + 1, :], jnp.asarray(block + 1, BF16), found)
+    found = found.astype(F32)
     hit = (found > 0.0).astype(F32)
     block_of = (found - hit).astype(BF16)
     ones = jnp.ones((8, LANES), BF16)
@@ -55,67 +57,70 @@
 
 
 def prepare_kernel(
-    own, ids_hbm, old_hbm, new_hbm, book_hbm, vec_hbm, rot_hbm, cent_hbm,
-    turned_ref, digit_ref, code_ref, rot_ref, mine_ref, ids_ref, old_ref, new_ref, book_ref, vec_ref, arrived,
+    own, ids_hbm, old_hbm, new_hbm, vec_hbm, rot_hbm, cent_hbm, book_hbm,
+    turned_ref, digit_ref, rot_ref, mine_ref, book_ref, ids_ref, old_ref, new_ref, vec_ref, arrived,
 ):
-    first = lax.axis_index("gx") * own
     side = lax.axis_index("gy")
     moves = (
         (ids_hbm, ids_ref),
         (old_hbm, old_ref),
         (new_hbm, new_ref),
-        (book_hbm.at[pl.ds(first, own)], book_ref),
         (vec_hbm, vec_ref),
         (rot_hbm, rot_ref),
         (cent_hbm.at[pl.ds(side * LANES, LANES)], mine_ref),
+        (book_hbm.at[pl.ds(lax.axis_index("gx") * own, own)], book_ref),
     )
     copies = [pltpu.make_async_copy(src, dst, arrived.at[n]) for n, (src, dst) in enumerate(moves)]
     for copy in copies:
         copy.start()
     for copy in copies[:3]:
         copy.wait()
-    ids_across = jnp.broadcast_to(ids_ref[...], (LANES, LANES)).astype(F32).T.astype(jnp.int32)
+    ids_across = jnp.broadcast_to(ids_ref[...], (LANES, LANES)).astype(F32).T.astype(jnp.int32).astype(jnp.int16)
     old_high, old_low = slot_digits(ids_across, old_ref)
     new_high, new_low = slot_digits(ids_across, new_ref)
     row = lax.broadcasted_iota(jnp.int32, (8, LANES), 0)
     digits = jnp.where(row == 0, old_high, jnp.where(row == 1, old_low, jnp.where(row == 2, new_high, new_low)))
     digit_ref[...] = digits.astype(BF16)
     copies[3].wait()
-    codes = book_ref.shape[2]
-    row = lax.broadcasted_iota(jnp.int32, (8, codes), 0)
+    copies[4].wait()
+    turned_ref[...] = dot(vec_ref[...], rot_ref[...]).T.astype(BF16)
+    copies[5].wait()
+    copies[6].wait()
+
+
+def code_table(words):
+    own = len(words)
+    row = lax.broadcasted_iota(jnp.int32, words[0].shape, 0)
     parts, tails = [], []
-    for m in range(own):
-        words = book_ref[m].astype(F32)
-        zero = jnp.zeros_like(words)
-        parts.append(jnp.concatenate([-2.0 * words if n == m else zero for n in range(own)], axis=1))
-        norm = jnp.sum(words * words, axis=0, keepdims=True)
+    for m, word in enumerate(words):
+        zero = jnp.zeros_like(word)
+        parts.append(jnp.concatenate([-2.0 * word if n == m else zero for n in range(own)], axis=1))
+        norm = jnp.sum(word * word, axis=0, keepdims=True)
         top = norm.astype(BF16).astype(F32)
         middle = (norm - top).astype(BF16).astype(F32)
         low = norm - top - middle
         tails.append(jnp.where(row == 0, top, jnp.where(row == 1, middle, jnp.where(row == 2, low, 0.0))))
     parts.append(jnp.concatenate(tails, axis=1))
-    code_ref[...] = jnp.concatenate(parts, axis=0).T.astype(BF16)
-    copies[4].wait()
-    copies[5].wait()
-    turned_ref[...] = dot(vec_ref[...], rot_ref[...]).T.astype(BF16)
-    copies[6].wait()
-
-
-def pack_kernel(width, mine_ref, other_ref, rot_ref, turned_ref, digit_ref, out_ref):
+    return jnp.concatenate(parts, axis=0).T.astype(BF16)
+
+
+def pack_kernel(mine_ref, other_ref, rot_ref, turned_ref, digit_ref, book_ref, out_ref, code_ref):
     side = lax.axis_index("gy")
     half = mine_ref.shape[1]
+    own, sub_width = book_ref.shape[:2]
+    width = own * sub_width
     other = other_ref[pl.ds(side * LANES, LANES), :]
     rotated = dot(mine_ref[...], rot_ref[pl.ds(side * half, half), :])
     rotated += dot(other, rot_ref[pl.ds((1 - side) * half, half), :])
+    code_ref[...] = code_table([book_ref[m].astype(F32) for m in range(own)])
     cents = rotated.T
     vectors = turned_ref[...].astype(F32)
     digits = digit_ref[...].astype(F32)
     for device in range(out_ref.shape[0]):
-        at = (device % 2) * half + (device // 2) * width
         for part in range(width // 4):
-            rows = slice(at + 4 * part, at + 4 * part + 4)
-            out_ref[device, part] = vectors[rows].astype(BF16)
-            out_ref[device, width // 4 + part] = cents[rows].astype(BF16)
+            at = (device % 2) * half + (device // 2) * width + 4 * part
+            out_ref[device, part] = vectors[at : at + 4].astype(BF16)
+            out_ref[device, width // 4 + part] = cents[at : at + 4].astype(BF16)
         out_ref[device, width // 2] = digits[0:4].astype(BF16)
 
 
@@ -166,19 +171,18 @@
 
     def gather(tile, error, sums):
         pair = jnp.concatenate([digits[2 * tile], digits[2 * tile + 1]], axis=1)
-        top = error.astype(BF16).astype(F32)
-        pad = jnp.zeros((8 - 2 * own - 1, WIDE), F32)
         for side in range(2):
-            out_ref[2 * tile + side, 0] = jnp.concatenate([top, error - top], axis=0)[
-                0:4, side * LANES : (side + 1) * LANES
-            ].astype(BF16)
-        rows = jnp.concatenate([top, error - top, jnp.ones((1, WIDE), F32), pad], axis=0)
-        high = jnp.broadcast_to(pair[2:3], (8, WIDE))
-        spread = jnp.concatenate([jnp.where(high == float(group), rows, 0.0) for group in range(tiles)], axis=0)
+            out_ref[2 * tile + side, 0] = error[0:2, side * LANES : (side + 1) * LANES].astype(BF16)
+        rows = jnp.concatenate([error, jnp.ones((1, WIDE), F32)] * 2, axis=0)
+        high = jnp.broadcast_to(pair[2:3], (8, WIDE)) - upper
+        spread = jnp.concatenate(
+            [jnp.where(high == float(group), rows, 0.0) for group in range(0, tiles, 2)], axis=0
+        )
         hot = (pair[3:4] == lane).astype(F32).astype(BF16)
         return sums + dot(spread.astype(BF16), hot, ((1,), (1,)))
 
-    sums = jnp.zeros((tiles * 8, WIDE), F32)
+    upper = (lax.broadcasted_iota(jnp.int32, (8, WIDE), 0) >= 4).astype(F32)
+    sums = jnp.zeros((tiles * 4, WIDE), F32)
     errors = []
     squares = [turn(0), turn(1)]
     for tile in range(tiles):
@@ -188,14 +192,19 @@
             sums = gather(tile - 1, errors[tile - 1], sums)
         squares = ahead
     sums = gather(tiles - 1, errors[tiles - 1], sums)
+    spare = jnp.zeros((1, LANES), BF16)
     for tile in range(tiles):
-        group = sums[tile * 8 : (tile + 1) * 8]
-        total = group[0:own] + group[own : 2 * own]
-        mean = total / jnp.maximum(group[2 * own : 2 * own + 1], 1.0)
-        pad = jnp.zeros((out_ref.shape[2] - own, LANES), F32)
+        group = sums[tile * 4 : (tile + 1) * 4]
+        mean = group[0:own] / jnp.maximum(group[own : own + 1], 1.0)
+        left, right = mean[:, :LANES], mean[:, LANES:]
+        last = jnp.concatenate([right[2:own].astype(BF16), spare], axis=0)
         for side in range(2):
-            for part, rows in enumerate((mean[:, :LANES], mean[:, LANES:])):
-                out_ref[2 * tile + side, part + 1] = jnp.concatenate([rows, pad], axis=0).astype(BF16)
+            device = 2 * tile + side
+            error = errors[tile][2:own, side * LANES : (side + 1) * LANES]
+            out_ref[device, 1] = left[0:2].astype(BF16)
+            out_ref[device, 2] = right[0:2].astype(BF16)
+            out_ref[device, 3] = jnp.concatenate([error, left[2:own]], axis=0).astype(BF16)
+            out_ref[device, 4] = last
 
 
 def finish_kernel(own, in_ref, quant_ref, list_ref):
@@ -203,11 +212,14 @@
     side = lax.axis_index("gy")
     for device in range(2 * tiles):
         at = ((device % 2) * tiles + device // 2) * own
-        quant_ref[at : at + own, :] = in_ref[device, 0].astype(F32)[0:own]
+        quant_ref[at : at + 2, :] = in_ref[device, 0].astype(F32)
+        quant_ref[at + 2 : at + own, :] = in_ref[device, 3].astype(F32)[0:1]
     for tile in range(tiles):
-        at = tile * own
-        list_ref[at : at + own, 0:LANES] = in_ref[2 * tile + side, 1].astype(F32)[0:own]
-        list_ref[at : at + own, LANES:WIDE] = in_ref[2 * tile + side, 2].astype(F32)[0:own]
+        at, device = tile * own, 2 * tile + side
+        list_ref[at : at + 2, 0:LANES] = in_ref[device, 1].astype(F32)
+        list_ref[at : at + 2, LANES:WIDE] = in_ref[device, 2].astype(F32)
+        list_ref[at + 2 : at + own, 0:LANES] = in_ref[device, 3].astype(F32)[1:2]
+        list_ref[at + 2 : at + own, LANES:WIDE] = in_ref[device, 4].astype(F32)[0:1]
 
 
 def on_device_by_column(vectors, list_ids, old_order, new_order, centroids, rotation, codebook):
@@ -219,14 +231,14 @@
     features = vectors.shape[1]
     total = subspaces * sides
     other = lax.ppermute(centroids, "gy", [(0, 1), (1, 0)])
-    turned, digits, code, rotation, mine = pl.pallas_call(
+    turned, digits, rotation, mine, book = pl.pallas_call(
         functools.partial(prepare_kernel, own),
         out_shape=(
             pltpu.VMEM((features, LANES), BF16),
             pltpu.VMEM((8, LANES), BF16),
-            pltpu.VMEM((own * codes, width + 8), BF16),
             pltpu.VMEM(rotation.shape, BF16),
             pltpu.VMEM((LANES, centroids.shape[1]), BF16),
+            pltpu.VMEM((own, sub_width, codes), BF16),
         ),
         in_specs=[pl.BlockSpec(memory_space=pl.ANY)] * 7,
         out_specs=(VMEM,) * 5,
@@ -234,7 +246,6 @@
             pltpu.VMEM((1, LANES), jnp.int32),
             pltpu.VMEM((old_order.shape[0] // LANES, LANES), jnp.int32),
             pltpu.VMEM((old_order.shape[0] // LANES, LANES), jnp.int32),
-            pltpu.VMEM((own, sub_width, codes), BF16),
             pltpu.VMEM((LANES, features), BF16),
             pltpu.SemaphoreType.DMA((7,)),
         ],
@@ -243,22 +254,25 @@
         list_ids.reshape(1, LANES),
         old_order.reshape(-1, LANES),
         new_order.reshape(-1, LANES),
-        codebook,
         vectors,
         rotation,
         centroids,
-    )
-    outgoing = pl.pallas_call(
-        functools.partial(pack_kernel, width),
-        out_shape=pltpu.VMEM((devices, width // 2 + 1, 4, LANES), BF16),
-        in_specs=[VMEM] * 5,
-        out_specs=VMEM,
+        codebook,
+    )
+    outgoing, code = pl.pallas_call(
+        pack_kernel,
+        out_shape=(
+            pltpu.VMEM((devices, width // 2 + 1, 4, LANES), BF16),
+            pltpu.VMEM((own * codes, width + 8), BF16),
+        ),
+        in_specs=[VMEM] * 6,
+        out_specs=(VMEM, VMEM),
         name="pack",
-    )(*(on_chip(array) for array in (mine, other, rotation, turned, digits)))
+    )(*(on_chip(array) for array in (mine, other, rotation, turned, digits, book)))
     incoming = lax.all_to_all(outgoing, ("gx", "gy"), split_axis=0, concat_axis=0, tiled=True)
     returning = pl.pallas_call(
         functools.partial(encode_kernel, own, sub_width),
-        out_shape=pltpu.VMEM((devices, 3, 4, LANES), BF16),
+        out_shape=pltpu.VMEM((devices, 5, 2, LANES), BF16),
         scratch_shapes=[
             pltpu.VMEM((owners, 2 * width, LANES), BF16),
             pltpu.VMEM((devices, width + 8, LANES), BF16),
@@ -288,7 +302,7 @@
     by_column = (
         sides == 2
         and own * owners == subspaces
-        and 1 <= own <= 3
+        and own == 3
         and sub_width == 8
         and codes % LANES == 0
         and vectors.shape[0] == LANES

time: 38.4 us -> 38.2 us (level)
  no operation moved by 1% of the time
where the time goes in v6:
time: 38.2 us; the launch traced here: 38 us
  blocking collectives  30.6 us (80%)
  Pallas kernels  6.14 us (16%)
  between operations  0.67 us (2%)
  starting transfers between devices  0.56 us (1%)
    all_to_all x1, blocking collectives, on_device_by_column(): lax.all_to_all(outgoing, ('gx', 'gy'), split_axis=0, concat_axis=0, tiled...  20.6 us
    all_to_all x1, blocking collectives, on_device_by_column(): lax.all_to_all(returning, ('gx', 'gy'), split_axis=0, concat_axis=0, tile...  10 us
    pallas_call x1, Pallas kernels, on_device_by_column(): pl.pallas_call(functools.partial(encode_kernel, own, sub_width), out_shap...  3.01 us
    pallas_call x1, Pallas kernels, on_device_by_column(): pl.pallas_call(functools.partial(prepare_kernel, own), out_shape=(pltpu.V...  1.94 us
  transfers between devices with their start and end apart: 1, of which 0 were waited for; matrix products, arithmetic and copies ran while one was open for 0% of the time, Pallas kernels for 5%

profile of v6, /device:TPU:0, one launch (start us, length us, event | category | flops | bytes accessed | tf_op | source)
XLA Modules:
  0.0 38.0 jit_solution(2996280481571199341)
XLA Ops:
  0.6 0.6 %collective-permute-start = (bf16[256,384]{1,0:T(8,128)(2,1)}, bf16[256,384]{1,0:T(8,128)(2,1)S(1)}, u32[]{:S(2)}, u32[]{:S(2)}) collective-permute-start(bf16[256,384]{1,0:T(8,128)(2,1)} %cent_hbm.1), channel_id=1, source_target_pairs={{0,1},{1,0},{2,3},{3,2},{4,5},{5,4},{6,7},{7,6},{8,9},{9,8},{10,11... | collective-permute-start | bytes 589832 | tf_op jit(solution)/shard_map/ppermute | solution.py:233
  1.2 1.9 %prepare.1 = (bf16[768,128]{1,0:T(8,128)(2,1)S(1)}, bf16[8,128]{1,0:T(8,128)(2,1)S(1)}, bf16[768,768]{1,0:T(8,128)(2,1)S(1)}, bf16[128,384]{1,0:T(8,128)(2,1)S(1)}, bf16[3,8,256]{2,1,0:T(8,128)(2,1)S(1)}) custom-call(s32[1,128]{1,0:T(1,128)} %bitcast.7, s32[32,128]{1,0:T(8,128)} %bitcast.5, s32[32,128]{1,0:T(8,128)} %bitcast.6, bf16[128,768]{1,0:T(8,128)(2,1)} %vec_hbm.1, ...), custom_call_target="tpu_custom_call" | custom-call | tf_op jit(solution)/shard_map/prepare/pallas_call | solution.py:234
  3.1 0.0 collective-permute-done.other_ref
  3.2 0.5 %pack.1 = (bf16[32,13,4,128]{3,2,1,0:T(4,128)(2,1)S(1)}, bf16[768,32]{1,0:T(8,128)(2,1)S(1)}) custom-call(bf16[128,384]{1,0:T(8,128)(2,1)S(1)} %get-tuple-element.11.mine_ref, bf16[256,384]{1,0:T(8,128)(2,1)S(1)} %collective-permute-done.other_ref, bf16[768,768]{1,0:T(8,128)(2,1)S(1)} %get-tuple-element.12.rot_ref, ...), custom_call_target="tpu_custom_call" | custom-call | tf_op jit(solution)/shard_map/pack/pallas_call | solution.py:262
  3.7 20.6 %all_to_all.10.in_ref = bf16[32,13,4,128]{3,2,1,0:T(4,128)(2,1)S(1)} all-to-all(bf16[32,13,4,128]{3,2,1,0:T(4,128)(2,1)S(1)} %get-tuple-element.16), channel_id=1, replica_groups=mesh['gx'=16,'gy'=2] {'gx','gy'}, dimensions={0} | all-to-all | bytes 851968 | tf_op jit(solution)/shard_map/all_to_all | solution.py:272
  24.3 3.0 %encode.1 = bf16[32,5,2,128]{3,2,1,0:T(2,128)(2,1)S(1)} custom-call(bf16[32,13,4,128]{3,2,1,0:T(4,128)(2,1)S(1)} %all_to_all.10.in_ref, bf16[768,32]{1,0:T(8,128)(2,1)S(1)} %get-tuple-element.17.code_ref), custom_call_target="tpu_custom_call" | custom-call | tf_op jit(solution)/shard_map/encode/pallas_call | solution.py:273
  27.3 10.0 %all_to_all.11.in_ref = bf16[32,5,2,128]{3,2,1,0:T(2,128)(2,1)S(1)} all-to-all(bf16[32,5,2,128]{3,2,1,0:T(2,128)(2,1)S(1)} %encode.1), channel_id=1, replica_groups=mesh['gx'=16,'gy'=2] {'gx','gy'}, dimensions={0} | all-to-all | bytes 163840 | tf_op jit(solution)/shard_map/all_to_all | solution.py:284
  37.3 0.7 %finish.1 = (f32[96,128]{1,0:T(8,128)}, f32[48,256]{1,0:T(8,128)}) custom-call(bf16[32,5,2,128]{3,2,1,0:T(2,128)(2,1)S(1)} %all_to_all.11.in_ref), custom_call_target="tpu_custom_call" | custom-call | tf_op jit(solution)/shard_map/finish/pallas_call | solution.py:285
Async XLA Ops:
  0.6 2.5 %collective-permute-start = (bf16[256,384]{1,0:T(8,128)(2,1)}, bf16[256,384]{1,0:T(8,128)(2,1)S(1)}, u32[]{:S(2)}, u32[]{:S(2)}) collective-permute-start(bf16[256,384]{1,0:T(8,128)(2,1)} %cent_hbm.1), channel_id=1, source_target_pairs={{0,1},{1,0},{2,3},{3,2},{4,5},{5,4},{6,7},{7,6},{8,9},{9,8},{10,11... | collective-permute-start | bytes 589832 | tf_op jit(solution)/shard_map/ppermute | solution.py:233

commit v7 on v6

--- a/solution.py
+++ b/solution.py
@@ -58,15 +58,15 @@
 
 def prepare_kernel(
     own, ids_hbm, old_hbm, new_hbm, vec_hbm, rot_hbm, cent_hbm, book_hbm,
-    turned_ref, digit_ref, rot_ref, mine_ref, book_ref, ids_ref, old_ref, new_ref, vec_ref, arrived,
+    vec_ref, digit_ref, rot_ref, mine_ref, book_ref, ids_ref, old_ref, new_ref, arrived,
 ):
     side = lax.axis_index("gy")
     moves = (
         (ids_hbm, ids_ref),
         (old_hbm, old_ref),
         (new_hbm, new_ref),
+        (rot_hbm, rot_ref),
         (vec_hbm, vec_ref),
-        (rot_hbm, rot_ref),
         (cent_hbm.at[pl.ds(side * LANES, LANES)], mine_ref),
         (book_hbm.at[pl.ds(lax.axis_index("gx") * own, own)], book_ref),
     )
@@ -81,11 +81,8 @@
     row = lax.broadcasted_iota(jnp.int32, (8, LANES), 0)
     digits = jnp.where(row == 0, old_high, jnp.where(row == 1, old_low, jnp.where(row == 2, new_high, new_low)))
     digit_ref[...] = digits.astype(BF16)
-    copies[3].wait()
-    copies[4].wait()
-    turned_ref[...] = dot(vec_ref[...], rot_ref[...]).T.astype(BF16)
-    copies[5].wait()
-    copies[6].wait()
+    for copy in copies[3:]:
+        copy.wait()
 
 
 def code_table(words):
@@ -104,17 +101,18 @@
     return jnp.concatenate(parts, axis=0).T.astype(BF16)
 
 
-def pack_kernel(mine_ref, other_ref, rot_ref, turned_ref, digit_ref, book_ref, out_ref, code_ref):
+def pack_kernel(mine_ref, other_ref, rot_ref, vec_ref, digit_ref, book_ref, out_ref, code_ref):
     side = lax.axis_index("gy")
     half = mine_ref.shape[1]
     own, sub_width = book_ref.shape[:2]
     width = own * sub_width
-    other = other_ref[pl.ds(side * LANES, LANES), :]
-    rotated = dot(mine_ref[...], rot_ref[pl.ds(side * half, half), :])
-    rotated += dot(other, rot_ref[pl.ds((1 - side) * half, half), :])
+    rotated = jnp.zeros((2 * LANES, rot_ref.shape[1]), F32)
+    for at, cents in ((side, mine_ref[...]), (1 - side, other_ref[pl.ds(side * LANES, LANES), :])):
+        rows = jnp.concatenate([vec_ref[:, pl.ds(at * half, half)], cents], axis=0)
+        rotated += dot(rows, rot_ref[pl.ds(at * half, half), :])
     code_ref[...] = code_table([book_ref[m].astype(F32) for m in range(own)])
-    cents = rotated.T
-    vectors = turned_ref[...].astype(F32)
+    turned = rotated.T
+    vectors, cents = turned[:, :LANES], turned[:, LANES:]
     digits = digit_ref[...].astype(F32)
     for device in range(out_ref.shape[0]):
         for part in range(width // 4):
@@ -231,10 +229,10 @@
     features = vectors.shape[1]
     total = subspaces * sides
     other = lax.ppermute(centroids, "gy", [(0, 1), (1, 0)])
-    turned, digits, rotation, mine, book = pl.pallas_call(
+    vectors, digits, rotation, mine, book = pl.pallas_call(
         functools.partial(prepare_kernel, own),
         out_shape=(
-            pltpu.VMEM((features, LANES), BF16),
+            pltpu.VMEM((LANES, features), BF16),
             pltpu.VMEM((8, LANES), BF16),
             pltpu.VMEM(rotation.shape, BF16),
             pltpu.VMEM((LANES, centroids.shape[1]), BF16),
@@ -246,7 +244,6 @@
             pltpu.VMEM((1, LANES), jnp.int32),
             pltpu.VMEM((old_order.shape[0] // LANES, LANES), jnp.int32),
             pltpu.VMEM((old_order.shape[0] // LANES, LANES), jnp.int32),
-            pltpu.VMEM((LANES, features), BF16),
             pltpu.SemaphoreType.DMA((7,)),
         ],
         name="prepare",
@@ -268,7 +265,7 @@
         in_specs=[VMEM] * 6,
         out_specs=(VMEM, VMEM),
         name="pack",
-    )(*(on_chip(array) for array in (mine, other, rotation, turned, digits, book)))
+    )(*(on_chip(array) for array in (mine, other, rotation, vectors, digits, book)))
     incoming = lax.all_to_all(outgoing, ("gx", "gy"), split_axis=0, concat_axis=0, tiled=True)
     returning = pl.pallas_call(
         functools.partial(encode_kernel, own, sub_width),
@@ -308,7 +305,8 @@
         and vectors.shape[0] == LANES
         and centroids.shape[0] == WIDE
         and old_order.shape[0] == owners * WIDE
-        and owners <= WIDE
+        and owners <= LANES
+        and owners % 2 == 0
     )
     plan = on_device_by_column if by_column else on_device_by_owner
     return plan(vectors, list_ids, old_order, new_order, centroids, rotation, codebook)

time: 38.2 us -> 38 us (level)
    pallas_call x1, Pallas kernels: 1.94 us -> 1.42 us  [on_device_by_column(): pl.pallas_call(functools.partial(prepare_kernel, own), out_shape=(pltpu.V...]
  transfers between devices with their start and end apart: 1 -> 1, of which waited for: 0 -> 0; matrix products, arithmetic and copies ran while one was open for 0% -> 0% of each run, Pallas kernels for 5% -> 4%
where the time goes in v7:
time: 38 us; the launch traced here: 37.8 us
  blocking collectives  30.7 us (81%)
  Pallas kernels  5.81 us (15%)
  between operations  0.66 us (2%)
  starting transfers between devices  0.56 us (1%)
    all_to_all x1, blocking collectives, on_device_by_column(): lax.all_to_all(outgoing, ('gx', 'gy'), split_axis=0, concat_axis=0, tiled...  20.7 us
    all_to_all x1, blocking collectives, on_device_by_column(): lax.all_to_all(returning, ('gx', 'gy'), split_axis=0, concat_axis=0, tile...  10 us
    pallas_call x1, Pallas kernels, on_device_by_column(): pl.pallas_call(functools.partial(encode_kernel, own, sub_width), out_shap...  3.01 us
    pallas_call x1, Pallas kernels, on_device_by_column(): pl.pallas_call(functools.partial(prepare_kernel, own), out_shape=(pltpu.V...  1.42 us
  transfers between devices with their start and end apart: 1, of which 0 were waited for; matrix products, arithmetic and copies ran while one was open for 0% of the time, Pallas kernels for 4%

profile of v7, /device:TPU:0, one launch (start us, length us, event | category | flops | bytes accessed | tf_op | source)
XLA Modules:
  0.0 37.8 jit_solution(10009824944219306866)
XLA Ops:
  0.6 0.6 %collective-permute-start = (bf16[256,384]{1,0:T(8,128)(2,1)}, bf16[256,384]{1,0:T(8,128)(2,1)S(1)}, u32[]{:S(2)}, u32[]{:S(2)}) collective-permute-start(bf16[256,384]{1,0:T(8,128)(2,1)} %cent_hbm.1), channel_id=1, source_target_pairs={{0,1},{1,0},{2,3},{3,2},{4,5},{5,4},{6,7},{7,6},{8,9},{9,8},{10,11... | collective-permute-start | bytes 589832 | tf_op jit(solution)/shard_map/ppermute | solution.py:231
  1.2 1.4 %prepare.1 = (bf16[128,768]{1,0:T(8,128)(2,1)S(1)}, bf16[8,128]{1,0:T(8,128)(2,1)S(1)}, bf16[768,768]{1,0:T(8,128)(2,1)S(1)}, bf16[128,384]{1,0:T(8,128)(2,1)S(1)}, bf16[3,8,256]{2,1,0:T(8,128)(2,1)S(1)}) custom-call(s32[1,128]{1,0:T(1,128)} %bitcast.7, s32[32,128]{1,0:T(8,128)} %bitcast.5, s32[32,128]{1,0:T(8,128)} %bitcast.6, bf16[128,768]{1,0:T(8,128)(2,1)} %vec_hbm.1, ...), custom_call_target="tpu_custom_call" | custom-call | tf_op jit(solution)/shard_map/prepare/pallas_call | solution.py:232
  2.6 0.0 collective-permute-done.other_ref
  2.6 0.7 %pack.1 = (bf16[32,13,4,128]{3,2,1,0:T(4,128)(2,1)S(1)}, bf16[768,32]{1,0:T(8,128)(2,1)S(1)}) custom-call(bf16[128,384]{1,0:T(8,128)(2,1)S(1)} %get-tuple-element.11.mine_ref, bf16[256,384]{1,0:T(8,128)(2,1)S(1)} %collective-permute-done.other_ref, bf16[768,768]{1,0:T(8,128)(2,1)S(1)} %get-tuple-element.12.rot_ref, ...), custom_call_target="tpu_custom_call" | custom-call | tf_op jit(solution)/shard_map/pack/pallas_call | solution.py:259
  3.3 20.7 %all_to_all.10.in_ref = bf16[32,13,4,128]{3,2,1,0:T(4,128)(2,1)S(1)} all-to-all(bf16[32,13,4,128]{3,2,1,0:T(4,128)(2,1)S(1)} %get-tuple-element.16), channel_id=1, replica_groups=mesh['gx'=16,'gy'=2] {'gx','gy'}, dimensions={0} | all-to-all | bytes 851968 | tf_op jit(solution)/shard_map/all_to_all | solution.py:269
  24.0 3.0 %encode.1 = bf16[32,5,2,128]{3,2,1,0:T(2,128)(2,1)S(1)} custom-call(bf16[32,13,4,128]{3,2,1,0:T(4,128)(2,1)S(1)} %all_to_all.10.in_ref, bf16[768,32]{1,0:T(8,128)(2,1)S(1)} %get-tuple-element.17.code_ref), custom_call_target="tpu_custom_call" | custom-call | tf_op jit(solution)/shard_map/encode/pallas_call | solution.py:270
  27.0 10.0 %all_to_all.11.in_ref = bf16[32,5,2,128]{3,2,1,0:T(2,128)(2,1)S(1)} all-to-all(bf16[32,5,2,128]{3,2,1,0:T(2,128)(2,1)S(1)} %encode.1), channel_id=1, replica_groups=mesh['gx'=16,'gy'=2] {'gx','gy'}, dimensions={0} | all-to-all | bytes 163840 | tf_op jit(solution)/shard_map/all_to_all | solution.py:281
  37.1 0.7 %finish.1 = (f32[96,128]{1,0:T(8,128)}, f32[48,256]{1,0:T(8,128)}) custom-call(bf16[32,5,2,128]{3,2,1,0:T(2,128)(2,1)S(1)} %all_to_all.11.in_ref), custom_call_target="tpu_custom_call" | custom-call | tf_op jit(solution)/shard_map/finish/pallas_call | solution.py:282
Async XLA Ops:
  0.6 2.0 %collective-permute-start = (bf16[256,384]{1,0:T(8,128)(2,1)}, bf16[256,384]{1,0:T(8,128)(2,1)S(1)}, u32[]{:S(2)}, u32[]{:S(2)}) collective-permute-start(bf16[256,384]{1,0:T(8,128)(2,1)} %cent_hbm.1), channel_id=1, source_target_pairs={{0,1},{1,0},{2,3},{3,2},{4,5},{5,4},{6,7},{7,6},{8,9},{9,8},{10,11... | collective-permute-start | bytes 589832 | tf_op jit(solution)/shard_map/ppermute | solution.py:231

commit v8 on v7

--- a/solution.py
+++ b/solution.py
@@ -182,14 +182,15 @@
     upper = (lax.broadcasted_iota(jnp.int32, (8, WIDE), 0) >= 4).astype(F32)
     sums = jnp.zeros((tiles * 4, WIDE), F32)
     errors = []
-    squares = [turn(0), turn(1)]
+    squares = [[turn(0), turn(1)]]
     for tile in range(tiles):
-        ahead = [turn(2 * tile + 2), turn(2 * tile + 3)] if tile + 1 < tiles else None
-        errors.append(measure(tile, squares))
-        if tile:
-            sums = gather(tile - 1, errors[tile - 1], sums)
-        squares = ahead
-    sums = gather(tiles - 1, errors[tiles - 1], sums)
+        if tile + 1 < tiles:
+            squares.append([turn(2 * tile + 2), turn(2 * tile + 3)])
+        errors.append(measure(tile, squares[tile]))
+        if tile > 1:
+            sums = gather(tile - 2, errors[tile - 2], sums)
+    for tile in (tiles - 2, tiles - 1):
+        sums = gather(tile, errors[tile], sums)
     spare = jnp.zeros((1, LANES), BF16)
     for tile in range(tiles):
         group = sums[tile * 4 : (tile + 1) * 4]

time: 38 us -> 37.9 us (level)
  no operation moved by 1% of the time
where the time goes in v8:
time: 37.9 us; the launch traced here: 37.7 us
  blocking collectives  30.7 us (81%)
  Pallas kernels  5.76 us (15%)
  between operations  0.66 us (2%)
  starting transfers between devices  0.56 us (1%)
    all_to_all x1, blocking collectives, on_device_by_column(): lax.all_to_all(outgoing, ('gx', 'gy'), split_axis=0, concat_axis=0, tiled...  20.7 us
    all_to_all x1, blocking collectives, on_device_by_column(): lax.all_to_all(returning, ('gx', 'gy'), split_axis=0, concat_axis=0, tile...  10 us
    pallas_call x1, Pallas kernels, on_device_by_column(): pl.pallas_call(functools.partial(encode_kernel, own, sub_width), out_shap...  2.96 us
    pallas_call x1, Pallas kernels, on_device_by_column(): pl.pallas_call(functools.partial(prepare_kernel, own), out_shape=(pltpu.V...  1.42 us
  transfers between devices with their start and end apart: 1, of which 0 were waited for; matrix products, arithmetic and copies ran while one was open for 0% of the time, Pallas kernels for 4%

profile of v8, /device:TPU:0, one launch (start us, length us, event | category | flops | bytes accessed | tf_op | source)
XLA Modules:
  0.0 37.7 jit_solution(13277766306428435867)
XLA Ops:
  0.6 0.6 %collective-permute-start = (bf16[256,384]{1,0:T(8,128)(2,1)}, bf16[256,384]{1,0:T(8,128)(2,1)S(1)}, u32[]{:S(2)}, u32[]{:S(2)}) collective-permute-start(bf16[256,384]{1,0:T(8,128)(2,1)} %cent_hbm.1), channel_id=1, source_target_pairs={{0,1},{1,0},{2,3},{3,2},{4,5},{5,4},{6,7},{7,6},{8,9},{9,8},{10,11... | collective-permute-start | bytes 589832 | tf_op jit(solution)/shard_map/ppermute | solution.py:232
  1.2 1.4 %prepare.1 = (bf16[128,768]{1,0:T(8,128)(2,1)S(1)}, bf16[8,128]{1,0:T(8,128)(2,1)S(1)}, bf16[768,768]{1,0:T(8,128)(2,1)S(1)}, bf16[128,384]{1,0:T(8,128)(2,1)S(1)}, bf16[3,8,256]{2,1,0:T(8,128)(2,1)S(1)}) custom-call(s32[1,128]{1,0:T(1,128)} %bitcast.7, s32[32,128]{1,0:T(8,128)} %bitcast.5, s32[32,128]{1,0:T(8,128)} %bitcast.6, bf16[128,768]{1,0:T(8,128)(2,1)} %vec_hbm.1, ...), custom_call_target="tpu_custom_call" | custom-call | tf_op jit(solution)/shard_map/prepare/pallas_call | solution.py:233
  2.6 0.0 collective-permute-done.other_ref
  2.6 0.7 %pack.1 = (bf16[32,13,4,128]{3,2,1,0:T(4,128)(2,1)S(1)}, bf16[768,32]{1,0:T(8,128)(2,1)S(1)}) custom-call(bf16[128,384]{1,0:T(8,128)(2,1)S(1)} %get-tuple-element.11.mine_ref, bf16[256,384]{1,0:T(8,128)(2,1)S(1)} %collective-permute-done.other_ref, bf16[768,768]{1,0:T(8,128)(2,1)S(1)} %get-tuple-element.12.rot_ref, ...), custom_call_target="tpu_custom_call" | custom-call | tf_op jit(solution)/shard_map/pack/pallas_call | solution.py:260
  3.3 20.7 %all_to_all.10.in_ref = bf16[32,13,4,128]{3,2,1,0:T(4,128)(2,1)S(1)} all-to-all(bf16[32,13,4,128]{3,2,1,0:T(4,128)(2,1)S(1)} %get-tuple-element.16), channel_id=1, replica_groups=mesh['gx'=16,'gy'=2] {'gx','gy'}, dimensions={0} | all-to-all | bytes 851968 | tf_op jit(solution)/shard_map/all_to_all | solution.py:270
  24.0 3.0 %encode.1 = bf16[32,5,2,128]{3,2,1,0:T(2,128)(2,1)S(1)} custom-call(bf16[32,13,4,128]{3,2,1,0:T(4,128)(2,1)S(1)} %all_to_all.10.in_ref, bf16[768,32]{1,0:T(8,128)(2,1)S(1)} %get-tuple-element.17.code_ref), custom_call_target="tpu_custom_call" | custom-call | tf_op jit(solution)/shard_map/encode/pallas_call | solution.py:271
  27.0 10.0 %all_to_all.11.in_ref = bf16[32,5,2,128]{3,2,1,0:T(2,128)(2,1)S(1)} all-to-all(bf16[32,5,2,128]{3,2,1,0:T(2,128)(2,1)S(1)} %encode.1), channel_id=1, replica_groups=mesh['gx'=16,'gy'=2] {'gx','gy'}, dimensions={0} | all-to-all | bytes 163840 | tf_op jit(solution)/shard_map/all_to_all | solution.py:282
  37.0 0.7 %finish.1 = (f32[96,128]{1,0:T(8,128)}, f32[48,256]{1,0:T(8,128)}) custom-call(bf16[32,5,2,128]{3,2,1,0:T(2,128)(2,1)S(1)} %all_to_all.11.in_ref), custom_call_target="tpu_custom_call" | custom-call | tf_op jit(solution)/shard_map/finish/pallas_call | solution.py:283
Async XLA Ops:
  0.6 2.0 %collective-permute-start = (bf16[256,384]{1,0:T(8,128)(2,1)}, bf16[256,384]{1,0:T(8,128)(2,1)S(1)}, u32[]{:S(2)}, u32[]{:S(2)}) collective-permute-start(bf16[256,384]{1,0:T(8,128)(2,1)} %cent_hbm.1), channel_id=1, source_target_pairs={{0,1},{1,0},{2,3},{3,2},{4,5},{5,4},{6,7},{7,6},{8,9},{9,8},{10,11... | collective-permute-start | bytes 589832 | tf_op jit(solution)/shard_map/ppermute | solution.py:232
